TPU v7x, 32 devices: a whole 2x2x4 slice. The times are simulated.
32 devices in a mesh: rep: 2 (over x), head: 4 (over z), seq: 4 (over y, core).
Axes of the slice: x: 2, y: 2, z: 4, core: 2. Of those that a mesh axis runs over, the one named last changes fastest.
Arguments:
- tokens: bfloat16 [128, 8192], P('rep'), parts along dimension 0
- w_query: bfloat16 [8192, 8192], replicated
- w_key: bfloat16 [8192, 1024], replicated
- w_value: bfloat16 [8192, 1024], replicated
- w_out: bfloat16 [8192, 8192], P(('head', 'seq'))
- k_cache: bfloat16 [128, 1024, 8, 128], P('rep', 'seq', 'head'), parts along dimension 0
- v_cache: bfloat16 [128, 1024, 8, 128], P('rep', 'seq', 'head'), parts along dimension 0
- positions: int32 [128], P('rep'), parts along dimension 0
Outputs:
- output 1: bfloat16 [128, 8192], P('rep'), parts along dimension 0
- output 2: bfloat16 [128, 1024, 8, 128], P('rep', 'seq', 'head'), parts along dimension 0
- output 3: bfloat16 [128, 1024, 8, 128], P('rep', 'seq', 'head'), parts along dimension 0
There are 2 independent parts. A program takes and returns all parts, laid end to end along the dimension named above; an argument that names none is the same for every part.
All inputs are finite; a program needn't handle non-finite values.
Results may differ from a plain program's by a relative error of at most 0.00554661.
Values are sent between devices in bfloat16 or wider.
A program may use at most 1 GiB of HBM per device.

v0:
```python
import jax
import jax.numpy as jnp
from jax import lax
from jax.sharding import PartitionSpec as P


def solution(mesh):
    head_devs = mesh.shape['head']
    cache_spec = P('rep', 'seq', 'head', None)

    def local_step(tokens, w_query, w_key, w_value, w_out, k_cache, v_cache, positions):
        batch_size, shard_len, kv_local, head_dim = k_cache.shape
        heads_total = w_query.shape[1] // head_dim
        groups = heads_total // (kv_local * head_devs)
        q_cols = kv_local * groups * head_dim
        kv_cols = kv_local * head_dim
        wo_rows = w_out.shape[0]
        head_idx = lax.axis_index('head')
        seq_idx = lax.axis_index('seq')
        wq_local = lax.dynamic_slice_in_dim(w_query, head_idx * q_cols, q_cols, axis=1)
        wk_local = lax.dynamic_slice_in_dim(w_key, head_idx * kv_cols, kv_cols, axis=1)
        wv_local = lax.dynamic_slice_in_dim(w_value, head_idx * kv_cols, kv_cols, axis=1)
        query = jnp.dot(tokens, wq_local, preferred_element_type=jnp.float32).astype(jnp.bfloat16).reshape(batch_size, kv_local, groups, head_dim)
        new_key = jnp.dot(tokens, wk_local, preferred_element_type=jnp.float32).astype(jnp.bfloat16).reshape(batch_size, 1, kv_local, head_dim)
        new_value = jnp.dot(tokens, wv_local, preferred_element_type=jnp.float32).astype(jnp.bfloat16).reshape(batch_size, 1, kv_local, head_dim)
        slot_ids = seq_idx * shard_len + jnp.arange(shard_len, dtype=jnp.int32)
        is_slot = (slot_ids[None, :] == positions[:, None])[:, :, None, None]
        k_new = jnp.where(is_slot, new_key, k_cache)
        v_new = jnp.where(is_slot, new_value, v_cache)
        scores = jnp.einsum('bkgd,btkd->bkgt', query, k_new, preferred_element_type=jnp.float32) * head_dim ** -0.5
        valid_mask = (slot_ids[None, :] <= positions[:, None])[:, None, None, :]
        scores = jnp.where(valid_mask, scores, -jnp.inf)
        local_max = jnp.max(scores, axis=-1)
        safe_max = jnp.where(jnp.isfinite(local_max), local_max, 0.0)
        weights = jnp.exp(scores - safe_max[..., None])
        local_sum = jnp.sum(weights, axis=-1)
        local_mix = jnp.einsum('bkgt,btkd->bkgd', weights.astype(jnp.bfloat16), v_new, preferred_element_type=jnp.float32)
        global_max = lax.pmax(local_max, 'seq')
        rescale = jnp.exp(local_max - global_max)
        total_sum, total_mix = lax.psum((local_sum * rescale, local_mix * rescale[..., None]), 'seq')
        attn_flat = (total_mix / total_sum[..., None]).astype(jnp.bfloat16).reshape(batch_size, q_cols)
        attn_part = lax.dynamic_slice_in_dim(attn_flat, seq_idx * wo_rows, wo_rows, axis=1)
        y_part = jnp.dot(attn_part, w_out, preferred_element_type=jnp.float32)
        y_total = lax.psum(y_part, ('head', 'seq'))
        return y_total.astype(jnp.bfloat16), k_new, v_new

    return jax.shard_map(
        local_step,
        mesh=mesh,
        in_specs=(P('rep', None), P(), P(), P(), P(('head', 'seq'), None), cache_spec, cache_spec, P('rep')),
        out_specs=(P('rep', None), cache_spec, cache_spec),
        check_vma=False,
    )
```

profile of v0, /device:TPU:0, one launch (start us, length us, event | category | flops | bytes accessed | tf_op | source)
XLA Modules:
  0.0 199.2 jit_solution(4556919386857182577)
XLA Ops:
  7.2 0.0 copy-start
  7.2 0.0 all-reduce.3.cloned.1.call-start
  7.2 1.2 copy-done
  8.4 3.0 %fusion.34 = bf16[64,256]{1,0:T(8,128)(2,1)S(1)} fusion(bf16[64,8192]{1,0:T(8,128)(2,1)S(1)} %copy-done, bf16[8192,1024]{1,0:T(8,128)(2,1)} %param.10, s32[]{:T(128)S(6)} %select_n.30), kind=kOutput, calls=%fused_computation.20 | convolution fusion | flops 268451840 | bytes 5275652 | tf_op jit(solution)/shard_map/dot_general | solution.py:24
  11.4 3.0 %fusion.31 = bf16[64,256]{1,0:T(8,128)(2,1)S(1)} fusion(bf16[64,8192]{1,0:T(8,128)(2,1)S(1)} %copy-done, bf16[8192,1024]{1,0:T(8,128)(2,1)} %param.11, s32[]{:T(128)S(6)} %select_n.30), kind=kOutput, calls=%fused_computation.19 | convolution fusion | flops 268451840 | bytes 5275652 | tf_op jit(solution)/shard_map/dot_general | solution.py:25
  14.4 0.0 copy-start.3
  14.5 13.6 %fusion.22 = bf16[8,8,16,128]{3,1,2,0:T(8,128)(2,1)S(1)} fusion(bf16[64,8192]{1,0:T(8,128)(2,1)S(1)} %copy-done, bf16[8192,8192]{1,0:T(8,128)(2,1)} %param.9, s32[]{:T(128)S(6)} %select_n.29), kind=kOutput, calls=%fused_computation.16 | convolution fusion | flops 2147614720 | bytes 34865156 | tf_op jit(solution)/shard_map/dot_general | solution.py:23
  28.1 0.0 copy-done.3
  28.2 0.1 broadcast_compare_fusion.1
  28.2 25.6 %broadcast_select_fusion.1 = (bf16[64,256,2,128]{3,2,1,0:T(2,128)(2,1)S(1)}, bf16[64,256,2,128]{3,2,1,0:T(2,128)(2,1)}) fusion(bf16[64,256,2,128]{3,2,1,0:T(2,128)(2,1)} %param.13, pred[64,256]{1,0:T(8,128)(4,1)S(1)} %get-tuple-element.8, bf16[64,2,128]{2,1,0:T(2,128)(2,1)S(1)} %broadcast_in_dim.55, bf16[64,256,2,128]{3,2,1,0:T(2,128)(2,1)} %param.14, ...), kind=kLoop, calls=%fused_computation.3 | loop fusion | flops 8388608 | bytes 33636352 | tf_op jit(solution)/shard_map/jit(_where)/select_n | solution.py:28
  53.8 0.0 copy-start.2
  53.9 3.4 %copy-done.2 = bf16[64,256,2,128]{3,2,1,0:T(2,128)(2,1)} copy-done((bf16[64,256,2,128]{3,2,1,0:T(2,128)(2,1)}, bf16[64,256,2,128]{3,2,1,0:T(2,128)(2,1)S(1)}, u32[]{:S(2)}) %copy-start.2) | copy-done | bytes 8388632
  57.2 2.4 %fusion.48 = (f32[64,2,8]{2,1,0:T(2,128)S(1)}, f32[64,2,8,256]{3,2,1,0:T(8,128)S(1)}) fusion(bf16[64,2,8,128]{3,2,1,0:T(8,128)(2,1)S(1)} %bitcast.25, bf16[64,256,2,128]{3,2,1,0:T(2,128)(2,1)S(1)} %get-tuple-element.5, pred[64,256]{1,0:T(8,128)(4,1)S(1)} %get-tuple-element.7), kind=kOutput, calls=%fused_computation.39 | convolution fusion | flops 67894272 | bytes 9719808 | tf_op jit(solution)/shard_map/bkgd,btkd->bkgt/dot_general | solution.py:30
  59.7 13.5 %pmax.7 = f32[64,2,8]{2,1,0:T(2,128)S(1)} all-reduce(f32[64,2,8]{2,1,0:T(2,128)S(1)} %get-tuple-element.9), channel_id=1, replica_groups=mesh['rep'=2,'head'=4,'seq'=4] {'seq'}, use_global_device_ids=true, to_apply=%region_1.2 | all-reduce | flops 1024 | bytes 8192 | tf_op jit(solution)/shard_map/pmax | solution.py:38
  73.2 0.4 fusion.37
  73.7 5.5 %fusion.19 = f32[64,2,8,128]{3,2,1,0:T(8,128)} fusion(bf16[64,256,2,128]{3,2,1,0:T(2,128)(2,1)} %get-tuple-element.6, f32[64,2,8,256]{3,2,1,0:T(8,128)S(1)} %get-tuple-element.10, f32[64,2,8]{2,1,0:T(2,128)S(1)} %is-finite_select_fusion, f32[64,2,8]{2,1,0:T(2,128)S(1)} %bitcast.31), kind=kOutput, calls=%fused_computation.15 | convolution fusion | flops 67764224 | bytes 9969664 | tf_op jit(solution)/shard_map/bkgt,btkd->bkgd/dot_general | solution.py:37
  79.1 0.0 all-reduce.3.cloned.1.call-update
  79.2 11.1 %psum.22 = f32[64,2,8]{2,1,0:T(2,128)S(1)} all-reduce(f32[64,2,8]{2,1,0:T(2,128)S(1)} %bitcast.29), channel_id=1, replica_groups=mesh['rep'=2,'head'=4,'seq'=4] {'seq'}, use_global_device_ids=true, to_apply=%region_4.5 | all-reduce | flops 1024 | bytes 8192 | tf_op jit(solution)/shard_map/psum | solution.py:40
  90.2 22.8 %all-reduce.3.cloned.1.call-done = f32[64,2,8,128]{3,2,1,0:T(8,128)} async-done(((f32[64,2,8,128]{3,2,1,0:T(8,128)}), f32[64,2,8,128]{3,2,1,0:T(8,128)}) %all-reduce.3.cloned.1.call-update) | async-done | bytes 524304 | tf_op jit(solution)/shard_map/psum | solution.py:40
  113.0 1.2 divide_convert_fusion
  114.3 0.1 copy.28
  114.3 0.0 copy-start.1
  114.4 5.0 %fusion.41 = f32[64,8192]{1,0:T(8,128)S(1)} fusion(bf16[512,8192]{1,0:T(8,128)(2,1)} %param.12, bf16[64,2048]{1,0:T(8,128)(2,1)S(1)} %bitcast.27, s32[]{:T(128)S(6)} %select_n.35), kind=kOutput, calls=%fused_computation.28 | convolution fusion | flops 536870912 | bytes 10551300 | tf_op jit(solution)/shard_map/dot_general | solution.py:43
  119.4 72.9 %all-reduce.4 = bf16[64,8192]{1,0:T(8,128)(2,1)} all-reduce(f32[64,8192]{1,0:T(8,128)S(1)} %fusion.41), channel_id=1, replica_groups=mesh['rep'=2,'head'=4,'seq'=4] {'head','seq'}, use_global_device_ids=true, to_apply=%region_5.6 | all-reduce | flops 524288 | bytes 3145728 | tf_op jit(solution)/shard_map/psum | solution.py:44
  192.3 0.0 copy-done.1
  (6 shorter events, 0.1 us)
Async XLA Ops:
  7.2 1.2 copy-start
  7.2 105.8 %all-reduce.3.cloned.1.call-start = ((), (), s32[]{:S(2)}) async-start(), calls=%async_computation | async-start | bytes 1048576 | tf_op jit(solution)/shard_map/psum | solution.py:40
  14.4 13.7 %copy-start.3 = (s32[64]{0:T(128)S(1)}, s32[64]{0:T(128)}, u32[]{:S(2)}) copy-start(s32[64]{0:T(128)} %param.15) | copy-start | bytes 772
  53.8 3.4 %copy-start.2 = (bf16[64,256,2,128]{3,2,1,0:T(2,128)(2,1)}, bf16[64,256,2,128]{3,2,1,0:T(2,128)(2,1)S(1)}, u32[]{:S(2)}) copy-start(bf16[64,256,2,128]{3,2,1,0:T(2,128)(2,1)S(1)} %get-tuple-element.5) | copy-start | bytes 25165828
  114.3 78.0 %copy-start.1 = (bf16[64,8192]{1,0:T(8,128)(2,1)S(1)}, bf16[64,8192]{1,0:T(8,128)(2,1)}, u32[]{:S(2)}) copy-start(bf16[64,8192]{1,0:T(8,128)(2,1)} %param.8) | copy-start | bytes 3145732
Sparse Core Ops, SparseCore 0:
  79.3 33.6 all-reduce.2
where the time goes:
time: 200 us; the launch traced here: 199 us
  blocking collectives  97.5 us (49%)
  matrix products  32.6 us (16%)
  other arithmetic  27.4 us (14%)
  waiting for transfers between devices  22.8 us (11%)
  between operations  14.2 us (7%)
  local copies, waits for them, and re-layouts  4.71 us (2%)
    psum x1, blocking collectives, local_step(): y_total = lax.psum(y_part, ('head', 'seq'))  72.9 us
    select_n x1, other arithmetic, local_step(): k_new = jnp.where(is_slot, new_key, k_cache)  25.6 us
    psum x1, waiting for transfers between devices, local_step(): lax.psum((local_sum * rescale, local_mix * rescale[..., None]), 'seq')  22.8 us
    dot_general x1, matrix products, local_step(): jnp.dot(tokens, wq_local, preferred_element_type=jnp.float32)  13.6 us
    pmax x1, blocking collectives, local_step(): global_max = lax.pmax(local_max, 'seq')  13.5 us
    psum x1, blocking collectives, local_step(): lax.psum((local_sum * rescale, local_mix * rescale[..., None]), 'seq')  11.1 us
    dot_general x1, matrix products, local_step(): jnp.einsum('bkgt,btkd->bkgd', weights.astype(jnp.bfloat16), v_new, prefer...  5.46 us
    dot_general x1, matrix products, local_step(): y_part = jnp.dot(attn_part, w_out, preferred_element_type=jnp.float32)  5.05 us
  transfers between devices with their start and end apart: 1, of which 1 were waited for; matrix products, arithmetic and copies ran while one was open for 0% of the time, Pallas kernels for 0%

commit v1 on v0

v1 whole, which is shorter than its diff:
```python
import functools

import jax
import jax.numpy as jnp
from jax import lax
from jax.experimental import pallas as pl
from jax.experimental.pallas import tpu as pltpu
from jax.sharding import PartitionSpec as P

MESH = pl.DeviceIdType.MESH
ANY = pl.BlockSpec(memory_space=pl.ANY)
VMEM = pl.BlockSpec(memory_space=pltpu.VMEM)
SMEM = pl.BlockSpec(memory_space=pltpu.SMEM)
N_SEQ = 4
N_HEAD = 4
LANES = 128
F32 = jnp.float32
BF16 = jnp.bfloat16


def entry_barrier(axes):
    sem = pltpu.get_barrier_semaphore()
    count = 0
    for axis, size in axes:
        me = lax.axis_index(axis)
        for step in range(1, size):
            pl.semaphore_signal(sem, inc=1, device_id={axis: lax.rem(me + step, size)}, device_id_type=MESH)
            count += 1
    return lambda: pl.semaphore_wait(sem, count)


def project_kernel(n_chunk, tok_hbm, wq_hbm, wk_hbm, wv_hbm, out, tok, wq, wkv, acc, acc_kv, stage, load_sem, send_sem, recv_sem):
    head, seq = lax.axis_index('head'), lax.axis_index('seq')
    q_cols, depth = wq.shape[2], wq.shape[1]
    n_q = q_cols // LANES
    batch = tok.shape[0]
    wait_peers = entry_barrier((('seq', N_SEQ),))

    q_at = pl.multiple_of((head * N_SEQ + seq) * q_cols, q_cols)
    kv_at = pl.multiple_of((head * 2 + lax.rem(seq, 2)) * LANES, LANES)

    def tok_copy(c):
        return pltpu.make_async_copy(tok_hbm.at[:, pl.ds(c * depth, depth)], tok.at[:, pl.ds(c * depth, depth)], load_sem.at[0, c])

    def q_copy(c):
        return pltpu.make_async_copy(wq_hbm.at[pl.ds(c * depth, depth), pl.ds(q_at, q_cols)], wq.at[c], load_sem.at[1, c])

    def kv_copy(src, c):
        return pltpu.make_async_copy(src.at[pl.ds(c * depth, depth), pl.ds(kv_at, LANES)], wkv.at[c], load_sem.at[2, c])

    for c in range(n_chunk):
        tok_copy(c).start()
        q_copy(c).start()

        @pl.when(seq < 2)
        def _():
            kv_copy(wk_hbm, c).start()

        @pl.when(seq >= 2)
        def _():
            kv_copy(wv_hbm, c).start()

    for c in range(n_chunk):
        tok_copy(c).wait()
        q_copy(c).wait()
        kv_copy(wk_hbm, c).wait()
        x = tok[:, c * depth:(c + 1) * depth]
        q_part = jnp.dot(x, wq[c], preferred_element_type=F32)
        kv_part = jnp.dot(x, wkv[c], preferred_element_type=F32)
        if c == 0:
            acc[...] = q_part
            acc_kv[...] = kv_part
        else:
            acc[...] += q_part
            acc_kv[...] += kv_part
    for i in range(n_q):
        stage[i] = acc[:, i * LANES:(i + 1) * LANES].astype(BF16)
    stage[n_q] = acc_kv[...].astype(BF16)

    wait_peers()
    copies = []
    for step in range(1, N_SEQ):
        copies.append(pltpu.make_async_remote_copy(
            src_ref=stage, dst_ref=out.at[seq], send_sem=send_sem.at[step - 1], recv_sem=recv_sem.at[step - 1],
            device_id={'seq': lax.rem(seq + step, N_SEQ)}, device_id_type=MESH))
        copies[-1].start()
    out[seq] = stage[...]
    for copy in copies:
        copy.wait()


def project(tokens, w_query, w_key, w_value):
    batch, d_model = tokens.shape
    q_cols = w_query.shape[1] // (N_HEAD * N_SEQ)
    n_chunk = 8
    depth = d_model // n_chunk
    n_q = q_cols // LANES
    return pl.pallas_call(
        functools.partial(project_kernel, n_chunk),
        out_shape=jax.ShapeDtypeStruct((N_SEQ, n_q + 1, batch, LANES), BF16),
        in_specs=[ANY] * 4,
        out_specs=VMEM,
        scratch_shapes=[
            pltpu.VMEM((batch, d_model), BF16),
            pltpu.VMEM((n_chunk, depth, q_cols), BF16),
            pltpu.VMEM((n_chunk, depth, LANES), BF16),
            pltpu.VMEM((batch, q_cols), F32),
            pltpu.VMEM((batch, LANES), F32),
            pltpu.VMEM((n_q + 1, batch, LANES), BF16),
            pltpu.SemaphoreType.DMA((3, n_chunk)),
            pltpu.SemaphoreType.DMA((N_SEQ - 1,)),
            pltpu.SemaphoreType.DMA((N_SEQ - 1,)),
        ],
        compiler_params=pltpu.CompilerParams(collective_id=0, has_side_effects=True),
        name='project',
    )(tokens, w_query, w_key, w_value)


def attend_kernel(n_chunk, shard_len, pos_ref, qkv_ref, k_hbm, v_hbm, k_out, v_out, mix_out, ml_out,
                  kbuf, vbuf, qf, kvf, load_sem, store_sem):
    batch, rows = kbuf.shape[0], kbuf.shape[1]
    n_q = qkv_ref.shape[1] - 1
    n_rows = N_SEQ * n_q
    per = batch // n_chunk
    start = lax.axis_index('seq') * shard_len

    def load(hbm, buf, which, c):
        return pltpu.make_async_copy(hbm.at[pl.ds(c * per, per)], buf.at[pl.ds(c * per, per)], load_sem.at[which, c])

    def store(hbm, buf, which, c):
        return pltpu.make_async_copy(buf.at[pl.ds(c * per, per)], hbm.at[pl.ds(c * per, per)], store_sem.at[which, c])

    for c in range(n_chunk):
        load(k_hbm, kbuf, 0, c).start()
        load(v_hbm, vbuf, 1, c).start()

    for s in range(N_SEQ):
        for i in range(n_q):
            at = (s * n_q + i) * batch
            qf[at:at + batch, :] = qkv_ref[s, i].astype(F32)
        kvf[s * batch:(s + 1) * batch, :] = qkv_ref[s, n_q].astype(F32)

    col = lax.broadcasted_iota(jnp.int32, (n_rows, rows), 1)
    row = lax.broadcasted_iota(jnp.int32, (n_rows, rows), 0)
    slot = jnp.where((col & 1) == row // (n_rows // 2), col >> 1, jnp.int32(1 << 30))
    win_row = lax.broadcasted_iota(jnp.int32, (16, LANES), 0)
    win_odd = (win_row & 1) == 1
    win_slot = win_row >> 1
    lane = lax.broadcasted_iota(jnp.int32, (n_rows, LANES), 1)

    def chunk(c, ml):
        load(k_hbm, kbuf, 0, c).wait()
        load(v_hbm, vbuf, 1, c).wait()
        for j in range(per):
            b = c * per + j
            pos = pos_ref[b] - start
            inside = jnp.logical_and(pos >= 0, pos < shard_len)
            slot_at = jnp.clip(pos, 0, shard_len - 1)
            base = pl.multiple_of((slot_at // 8) * 16, 16)
            hit = win_slot == jnp.where(inside, lax.rem(slot_at, 8), -1)
            for buf, first in ((kbuf, 0), (vbuf, 2)):
                new = jnp.where(win_odd, kvf[pl.ds((first + 1) * batch + b, 1), :], kvf[pl.ds(first * batch + b, 1), :])
                old = buf[b, pl.ds(base, 16), :]
                buf[b, pl.ds(base, 16), :] = jnp.where(hit, new.astype(BF16), old)
        for j in range(per):
            b = c * per + j
            limit = pos_ref[b] - start
            q = qf[pl.ds(b, n_rows, stride=batch), :].astype(BF16)
            s = lax.dot_general(q, kbuf[b], (((1,), (1,)), ((), ())), preferred_element_type=F32) * LANES ** -0.5
            s = jnp.where(slot <= limit, s, -jnp.inf)
            m = jnp.max(s, axis=1, keepdims=True)
            safe = jnp.where(m == -jnp.inf, 0.0, m)
            w = jnp.exp(s - safe)
            l = jnp.sum(w, axis=1, keepdims=True)
            mix = jnp.dot(w.astype(BF16), vbuf[b], preferred_element_type=F32)
            mix_out[pl.ds(b, n_rows, stride=batch), :] = mix
            ml = jnp.where(lane == b, m, jnp.where(lane == batch + b, l, ml))
        store(k_out, kbuf, 0, c).start()
        store(v_out, vbuf, 1, c).start()
        return ml

    ml = lax.fori_loop(0, n_chunk, chunk, jnp.zeros((n_rows, LANES), F32))
    ml_out[...] = jnp.zeros_like(ml_out)
    for s in range(N_SEQ):
        ml_out[s, 0:n_q, :] = ml[s * n_q:(s + 1) * n_q, :]
    for c in range(n_chunk):
        store(k_out, kbuf, 0, c).wait()
        store(v_out, vbuf, 1, c).wait()


def attend(positions, qkv, k_cache, v_cache, shard_len):
    batch, rows, _ = k_cache.shape
    n_rows = N_SEQ * (qkv.shape[1] - 1)
    n_chunk = 8
    cache = jax.ShapeDtypeStruct(k_cache.shape, BF16)
    return pl.pallas_call(
        functools.partial(attend_kernel, n_chunk, shard_len),
        out_shape=[cache, cache, jax.ShapeDtypeStruct((n_rows * batch, LANES), F32), jax.ShapeDtypeStruct((N_SEQ, 8, LANES), F32)],
        in_specs=[SMEM, VMEM, ANY, ANY],
        out_specs=[ANY, ANY, VMEM, VMEM],
        scratch_shapes=[
            pltpu.VMEM((batch, rows, LANES), BF16),
            pltpu.VMEM((batch, rows, LANES), BF16),
            pltpu.VMEM((n_rows * batch, LANES), F32),
            pltpu.VMEM((N_SEQ * batch, LANES), F32),
            pltpu.SemaphoreType.DMA((2, n_chunk)),
            pltpu.SemaphoreType.DMA((2, n_chunk)),
        ],
        name='attend',
    )(positions, qkv, k_cache, v_cache)


def output_kernel(mix, ml, wo_hbm, y, wo, mix_in, ml_in, attn, give, own, core_in, y_in, z_in,
                  wo_sem, a_send, a_recv, m_send, m_recv, c_send, c_recv, y_send, y_recv, z_send, z_recv,
                  gz_send, gz_recv, gy_send, gy_recv, gc_send, gc_recv):
    head, seq = lax.axis_index('head'), lax.axis_index('seq')
    side, core = seq // 2, lax.rem(seq, 2)
    partner = side * 2 + (1 - core)
    across = (1 - side) * 2 + core
    n_q, batch = mix_in.shape[1], mix_in.shape[2]
    width = own.shape[2]
    wait_peers = entry_barrier((('seq', N_SEQ), ('head', N_HEAD)))

    def place(k):
        half = (1 - core) if k < 8 else core
        quarter = (1 - side) if (k % 8) < 4 else side
        z = lax.rem(head + 2 + k % 4, N_HEAD)
        return half, quarter, z

    def column(half, quarter, z):
        return pl.multiple_of(((half * 2 + quarter) * N_HEAD + z) * width, width)

    def wo_copy(k):
        return pltpu.make_async_copy(wo_hbm.at[:, pl.ds(column(*place(k)), width)], wo.at[k], wo_sem.at[k])

    for k in range(16):
        wo_copy(k).start()

    def remote(src, dst, send, recv, device):
        return pltpu.make_async_remote_copy(src_ref=src, dst_ref=dst, send_sem=send, recv_sem=recv, device_id=device, device_id_type=MESH)

    wait_peers()
    a_copies = []
    for step in range(1, N_SEQ):
        to = lax.rem(seq + step, N_SEQ)
        a_copies.append(remote(ml.at[to], ml_in.at[step - 1], m_send.at[step - 1], m_recv.at[step - 1], {'seq': to}))
        a_copies.append(remote(mix.at[pl.ds(to * n_q, n_q)], mix_in.at[step - 1], a_send.at[step - 1], a_recv.at[step - 1], {'seq': to}))
    for copy in a_copies:
        copy.start()
    for copy in a_copies:
        copy.wait()

    parts = [ml[seq]] + [ml_in[i] for i in range(N_SEQ - 1)]
    top = functools.reduce(jnp.maximum, parts)
    scales = [jnp.exp(p - top) for p in parts]
    total = functools.reduce(jnp.add, [pltpu.roll(p, LANES - batch, 1) * e for p, e in zip(parts, scales)])
    scales = [e / total for e in scales]
    table = jnp.concatenate(scales + [jnp.zeros((LANES - 8 * N_SEQ, LANES), F32)], axis=0).T
    for i in range(n_q):
        acc = mix[seq * n_q + i] * table[0:batch, i:i + 1]
        for s in range(1, N_SEQ):
            acc += mix_in[s - 1, i] * table[0:batch, s * 8 + i:s * 8 + i + 1]
        attn[:, i * LANES:(i + 1) * LANES] = acc.astype(BF16)

    def partial(k):
        wo_copy(k).wait()
        return jnp.dot(attn[...], wo[k], preferred_element_type=F32)

    c_copies = []
    for k in range(8):
        give[k] = partial(k)
        c_copies.append(remote(give.at[k], core_in.at[k], c_send.at[k], c_recv.at[k], {'seq': partner}))
        c_copies[-1].start()
    y_copies = []
    for k in range(4):
        value = partial(8 + k)
        c_copies[k].wait_recv()
        own[k] = value + core_in[k]
        y_copies.append(remote(own.at[k], y_in.at[k], y_send.at[k], y_recv.at[k], {'seq': across}))
        y_copies[-1].start()
    for k in range(4):
        own[4 + k] = partial(12 + k)
    z_copies = []
    for k in range(4):
        c_copies[4 + k].wait_recv()
        y_copies[k].wait_recv()
        own[4 + k] = own[4 + k] + core_in[4 + k] + y_in[k]
        step = (2 + k) % 4
        if step:
            z_copies.append(remote(own.at[4 + k], z_in.at[step - 1], z_send.at[step - 1], z_recv.at[step - 1],
                                   {'head': lax.rem(head + step, N_HEAD)}))
            z_copies[-1].start()
        else:
            mine = 4 + k
    for copy in z_copies:
        copy.wait_recv()
    here = column(core, side, head)
    y[:, pl.ds(here, width)] = (own[mine] + z_in[0] + z_in[1] + z_in[2]).astype(BF16)

    def spread(half, quarter, z, send, recv, device):
        at = y.at[:, pl.ds(column(half, quarter, z), width)]
        return remote(at, at, send, recv, device)

    sends = []

    def go(copy):
        copy.start()
        sends.append(copy)

    gz, gy, gc = {}, {}, {}
    for step in (2, 1, 3):
        gz[step] = spread(core, side, head, gz_send.at[step - 1], gz_recv.at[step - 1], {'head': lax.rem(head + step, N_HEAD)})
        go(gz[step])
    gy[0] = spread(core, side, head, gy_send.at[0], gy_recv.at[0], {'seq': across})
    gc[0] = spread(core, side, head, gc_send.at[0], gc_recv.at[0], {'seq': partner})
    go(gy[0])
    go(gc[0])
    for step in (1, 3, 2):
        source = lax.rem(head + N_HEAD - step, N_HEAD)
        gz[step].wait_recv()
        gy[step] = spread(core, side, source, gy_send.at[step], gy_recv.at[step], {'seq': across})
        gc[step] = spread(core, side, source, gc_send.at[step], gc_recv.at[step], {'seq': partner})
        go(gy[step])
        go(gc[step])
    for step in (0, 1, 3, 2):
        source = lax.rem(head + N_HEAD - step, N_HEAD)
        gy[step].wait_recv()
        gc[4 + step] = spread(core, 1 - side, source, gc_send.at[4 + step], gc_recv.at[4 + step], {'seq': partner})
        go(gc[4 + step])
    for step in range(8):
        gc[step].wait_recv()
    for copy in a_copies[:0] + c_copies + y_copies + z_copies + sends:
        copy.wait_send()


def output(mix, ml, w_out):
    rows, d_out = w_out.shape
    n_q = rows // LANES
    batch = mix.shape[0] // (N_SEQ * n_q)
    width = d_out // 16
    dma = pltpu.SemaphoreType.DMA
    return pl.pallas_call(
        output_kernel,
        out_shape=jax.ShapeDtypeStruct((batch, d_out), BF16),
        in_specs=[VMEM, VMEM, ANY],
        out_specs=VMEM,
        scratch_shapes=[
            pltpu.VMEM((16, rows, width), BF16),
            pltpu.VMEM((3, n_q, batch, LANES), F32),
            pltpu.VMEM((3, 8, LANES), F32),
            pltpu.VMEM((batch, rows), BF16),
            pltpu.VMEM((8, batch, width), F32),
            pltpu.VMEM((8, batch, width), F32),
            pltpu.VMEM((8, batch, width), F32),
            pltpu.VMEM((4, batch, width), F32),
            pltpu.VMEM((3, batch, width), F32),
            dma((16,)),
            dma((3,)), dma((3,)), dma((3,)), dma((3,)),
            dma((8,)), dma((8,)), dma((4,)), dma((4,)), dma((3,)), dma((3,)),
            dma((3,)), dma((3,)), dma((4,)), dma((4,)), dma((8,)), dma((8,)),
        ],
        compiler_params=pltpu.CompilerParams(collective_id=1, has_side_effects=True),
        name='output',
    )(mix.reshape(N_SEQ * n_q, batch, LANES), ml, w_out)


def solution(mesh):
    cache_spec = P('rep', 'seq', 'head', None)

    def local_step(tokens, w_query, w_key, w_value, w_out, k_cache, v_cache, positions):
        batch, shard_len, kv_local, head_dim = k_cache.shape
        flat = (batch, shard_len * kv_local, head_dim)
        qkv = project(tokens, w_query, w_key, w_value)
        k_new, v_new, mix, ml = attend(positions, qkv, k_cache.reshape(flat), v_cache.reshape(flat), shard_len)
        y = output(mix, ml, w_out)
        return y, k_new.reshape(k_cache.shape), v_new.reshape(v_cache.shape)

    return jax.shard_map(
        local_step,
        mesh=mesh,
        in_specs=(P('rep', None), P(), P(), P(), P(('head', 'seq'), None), cache_spec, cache_spec, P('rep')),
        out_specs=(P('rep', None), cache_spec, cache_spec),
        check_vma=False,
    )
```

time: 200 us -> 81.8 us (0.41)
  blocking collectives: 97.5 us -> 0 us
  Pallas kernels: 0 us -> 78.7 us
  matrix products: 32.6 us -> 0 us
  other arithmetic: 27.4 us -> 0 us
  waiting for transfers between devices: 22.8 us -> 0 us
  between operations: 14.2 us -> 0.65 us
  local copies, waits for them, and re-layouts: 4.71 us -> 2.26 us
    psum x2 -> x0, blocking collectives: 84 us -> none  [the longest x1 72.9 us: local_step(): y_total = lax.psum(y_part, ('head', 'seq'))]
    pallas_call x0 -> x3, Pallas kernels: none -> 78.7 us  [the longest x1 45.9 us: output(): pl.pallas_call(output_kernel, out_shape=jax.ShapeDtypeStruct((batch, d_ou...]
    dot_general x6 -> x0, matrix products: 32.6 us -> none  [the longest x1 13.6 us: local_step(): jnp.dot(tokens, wq_local, preferred_element_type=jnp.float32)]
    select_n x2 -> x0, other arithmetic: 25.6 us -> none  [the longest x1 25.6 us: local_step(): k_new = jnp.where(is_slot, new_key, k_cache)]
    psum x1 -> x0, waiting for transfers between devices: 22.8 us -> none  [local_step(): lax.psum((local_sum * rescale, local_mix * rescale[..., None]), 'seq')]
    pmax x1 -> x0, blocking collectives: 13.5 us -> none  [local_step(): global_max = lax.pmax(local_max, 'seq')]
    unnamed x10 -> x1, local copies, waits for them, and re-layouts: 4.67 us -> 2.26 us
  transfers between devices with their start and end apart: 1 -> 0, of which waited for: 1 -> 0; matrix products, arithmetic and copies ran while one was open for 0% -> 0% of each run, Pallas kernels for 0% -> 0%
where the time goes in v1:
time: 81.8 us; the launch traced here: 81.6 us
  Pallas kernels  78.7 us (96%)
  local copies, waits for them, and re-layouts  2.26 us (3%)
    pallas_call x1, Pallas kernels, output(): pl.pallas_call(output_kernel, out_shape=jax.ShapeDtypeStruct((batch, d_ou...  45.9 us
    pallas_call x1, Pallas kernels, attend(): pl.pallas_call(functools.partial(attend_kernel, n_chunk, shard_len), out_...  20.6 us
    pallas_call x1, Pallas kernels, project(): pl.pallas_call(functools.partial(project_kernel, n_chunk), out_shape=jax....  12.1 us
    unnamed x1, local copies, waits for them, and re-layouts  2.26 us

profile of v1, /device:TPU:0, one launch (start us, length us, event | category | flops | bytes accessed | tf_op | source)
XLA Modules:
  0.0 81.6 jit_solution(8038833315253071029)
XLA Ops:
  0.6 12.1 %project.1.qkv_ref = bf16[4,5,64,128]{3,2,1,0:T(8,128)(2,1)} custom-call(bf16[64,8192]{1,0:T(8,128)(2,1)} %tok_hbm.1, bf16[8192,8192]{1,0:T(8,128)(2,1)} %wq_hbm.1, bf16[8192,1024]{1,0:T(8,128)(2,1)} %wk_hbm.1, bf16[8192,1024]{1,0:T(8,128)(2,1)} %wv_hbm.1), custom_call_target="tpu_custom_call" | custom-call | tf_op jit(solution)/shard_map/project/pallas_call | solution.py:98
  12.8 20.6 %attend.1 = (bf16[64,512,128]{2,1,0:T(8,128)(2,1)}, bf16[64,512,128]{2,1,0:T(8,128)(2,1)}, f32[1024,128]{1,0:T(8,128)}, f32[4,8,128]{2,1,0:T(8,128)}) custom-call(s32[64]{0:T(128)} %pos_ref.1, bf16[4,5,64,128]{3,2,1,0:T(8,128)(2,1)} %project.1.qkv_ref, bf16[64,512,128]{2,1,0:T(8,128)(2,1)} %bitcast.5, bf16[64,512,128]{2,1,0:T(8,128)(2,1)} %bitcast.6), custom_call_target="tpu_custom_call" | custom-call | tf_op jit(solution)/shard_map/attend/pallas_call | solution.py:196
  33.4 45.9 %output.1 = bf16[64,8192]{1,0:T(8,128)(2,1)} custom-call(f32[16,64,128]{2,1,0:T(8,128)} %bitcast.7, f32[4,8,128]{2,1,0:T(8,128)} %get-tuple-element.8.ml, bf16[512,8192]{1,0:T(8,128)(2,1)} %wo_hbm.1), custom_call_target="tpu_custom_call" | custom-call | tf_op jit(solution)/shard_map/output/pallas_call | solution.py:342
  79.3 2.3 %copy.12 = bf16[64,8192]{1,0:T(8,128)(2,1)} copy(bf16[64,8192]{1,0:T(8,128)(2,1)} %output.1) | data formatting | bytes 2097152

commit v2 on v1

--- a/solution.py
+++ b/solution.py
@@ -8,7 +8,7 @@
 from jax.sharding import PartitionSpec as P
 
 MESH = pl.DeviceIdType.MESH
-ANY = pl.BlockSpec(memory_space=pl.ANY)
+HBM = pl.BlockSpec(memory_space=pltpu.HBM)
 VMEM = pl.BlockSpec(memory_space=pltpu.VMEM)
 SMEM = pl.BlockSpec(memory_space=pltpu.SMEM)
 N_SEQ = 4
@@ -16,6 +16,10 @@
 LANES = 128
 F32 = jnp.float32
 BF16 = jnp.bfloat16
+
+
+def in_hbm(x):
+    return pltpu.with_memory_space_constraint(x, pltpu.HBM)
 
 
 def entry_barrier(axes):
@@ -29,7 +33,8 @@
     return lambda: pl.semaphore_wait(sem, count)
 
 
-def project_kernel(n_chunk, tok_hbm, wq_hbm, wk_hbm, wv_hbm, out, tok, wq, wkv, acc, acc_kv, stage, load_sem, send_sem, recv_sem):
+def project_kernel(n_chunk, ahead, tok_hbm, wq_hbm, wk_hbm, wv_hbm, k_hbm, v_hbm, out, kbuf, vbuf, tok, wq, wkv, acc, acc_kv, stage,
+                   load_sem, cache_sem, send_sem, recv_sem):
     head, seq = lax.axis_index('head'), lax.axis_index('seq')
     q_cols, depth = wq.shape[2], wq.shape[1]
     n_q = q_cols // LANES
@@ -48,7 +53,7 @@
     def kv_copy(src, c):
         return pltpu.make_async_copy(src.at[pl.ds(c * depth, depth), pl.ds(kv_at, LANES)], wkv.at[c], load_sem.at[2, c])
 
-    for c in range(n_chunk):
+    def start(c):
         tok_copy(c).start()
         q_copy(c).start()
 
@@ -60,7 +65,22 @@
         def _():
             kv_copy(wv_hbm, c).start()
 
+    caches = []
+    for g in range(8):
+        span = pl.ds(g * (batch // 8), batch // 8)
+        caches.append(pltpu.make_async_copy(k_hbm.at[span], kbuf.at[span], cache_sem.at[0, g]))
+        caches.append(pltpu.make_async_copy(v_hbm.at[span], vbuf.at[span], cache_sem.at[1, g]))
+    started = 0
+
+    for c in range(ahead):
+        start(c)
     for c in range(n_chunk):
+        if c + ahead < n_chunk:
+            start(c + ahead)
+        else:
+            for copy in caches[started:started + 4]:
+                copy.start()
+            started += 4
         tok_copy(c).wait()
         q_copy(c).wait()
         kv_copy(wk_hbm, c).wait()
@@ -87,19 +107,21 @@
     out[seq] = stage[...]
     for copy in copies:
         copy.wait()
-
-
-def project(tokens, w_query, w_key, w_value):
+    for copy in caches:
+        copy.wait()
+
+
+def project(tokens, w_query, w_key, w_value, k_cache, v_cache):
     batch, d_model = tokens.shape
     q_cols = w_query.shape[1] // (N_HEAD * N_SEQ)
     n_chunk = 8
     depth = d_model // n_chunk
     n_q = q_cols // LANES
     return pl.pallas_call(
-        functools.partial(project_kernel, n_chunk),
-        out_shape=jax.ShapeDtypeStruct((N_SEQ, n_q + 1, batch, LANES), BF16),
-        in_specs=[ANY] * 4,
-        out_specs=VMEM,
+        functools.partial(project_kernel, n_chunk, 4),
+        out_shape=[pltpu.VMEM((N_SEQ, n_q + 1, batch, LANES), BF16), pltpu.VMEM(k_cache.shape, BF16), pltpu.VMEM(k_cache.shape, BF16)],
+        in_specs=[HBM] * 6,
+        out_specs=[VMEM] * 3,
         scratch_shapes=[
             pltpu.VMEM((batch, d_model), BF16),
             pltpu.VMEM((n_chunk, depth, q_cols), BF16),
@@ -108,31 +130,25 @@
             pltpu.VMEM((batch, LANES), F32),
             pltpu.VMEM((n_q + 1, batch, LANES), BF16),
             pltpu.SemaphoreType.DMA((3, n_chunk)),
+            pltpu.SemaphoreType.DMA((2, 8)),
             pltpu.SemaphoreType.DMA((N_SEQ - 1,)),
             pltpu.SemaphoreType.DMA((N_SEQ - 1,)),
         ],
-        compiler_params=pltpu.CompilerParams(collective_id=0, has_side_effects=True),
+        compiler_params=pltpu.CompilerParams(collective_id=0, has_side_effects=True, vmem_limit_bytes=18 * 2**20),
         name='project',
-    )(tokens, w_query, w_key, w_value)
-
-
-def attend_kernel(n_chunk, shard_len, pos_ref, qkv_ref, k_hbm, v_hbm, k_out, v_out, mix_out, ml_out,
-                  kbuf, vbuf, qf, kvf, load_sem, store_sem):
+    )(*map(in_hbm, (tokens, w_query, w_key, w_value, k_cache, v_cache)))
+
+
+def attend_kernel(n_chunk, shard_len, pos_ref, qkv_ref, k_in, v_in, k_out, v_out, mix_out, ml_out, kbuf, vbuf,
+                  qf, kvf, store_sem):
     batch, rows = kbuf.shape[0], kbuf.shape[1]
     n_q = qkv_ref.shape[1] - 1
     n_rows = N_SEQ * n_q
     per = batch // n_chunk
     start = lax.axis_index('seq') * shard_len
 
-    def load(hbm, buf, which, c):
-        return pltpu.make_async_copy(hbm.at[pl.ds(c * per, per)], buf.at[pl.ds(c * per, per)], load_sem.at[which, c])
-
     def store(hbm, buf, which, c):
         return pltpu.make_async_copy(buf.at[pl.ds(c * per, per)], hbm.at[pl.ds(c * per, per)], store_sem.at[which, c])
-
-    for c in range(n_chunk):
-        load(k_hbm, kbuf, 0, c).start()
-        load(v_hbm, vbuf, 1, c).start()
 
     for s in range(N_SEQ):
         for i in range(n_q):
@@ -149,8 +165,6 @@
     lane = lax.broadcasted_iota(jnp.int32, (n_rows, LANES), 1)
 
     def chunk(c, ml):
-        load(k_hbm, kbuf, 0, c).wait()
-        load(v_hbm, vbuf, 1, c).wait()
         for j in range(per):
             b = c * per + j
             pos = pos_ref[b] - start
@@ -162,6 +176,8 @@
                 new = jnp.where(win_odd, kvf[pl.ds((first + 1) * batch + b, 1), :], kvf[pl.ds(first * batch + b, 1), :])
                 old = buf[b, pl.ds(base, 16), :]
                 buf[b, pl.ds(base, 16), :] = jnp.where(hit, new.astype(BF16), old)
+        store(k_out, kbuf, 0, c).start()
+        store(v_out, vbuf, 1, c).start()
         for j in range(per):
             b = c * per + j
             limit = pos_ref[b] - start
@@ -175,8 +191,6 @@
             mix = jnp.dot(w.astype(BF16), vbuf[b], preferred_element_type=F32)
             mix_out[pl.ds(b, n_rows, stride=batch), :] = mix
             ml = jnp.where(lane == b, m, jnp.where(lane == batch + b, l, ml))
-        store(k_out, kbuf, 0, c).start()
-        store(v_out, vbuf, 1, c).start()
         return ml
 
     ml = lax.fori_loop(0, n_chunk, chunk, jnp.zeros((n_rows, LANES), F32))
@@ -192,20 +206,20 @@
     batch, rows, _ = k_cache.shape
     n_rows = N_SEQ * (qkv.shape[1] - 1)
     n_chunk = 8
-    cache = jax.ShapeDtypeStruct(k_cache.shape, BF16)
+    cache = pltpu.HBM(k_cache.shape, BF16)
+    held = pltpu.VMEM(k_cache.shape, BF16)
     return pl.pallas_call(
         functools.partial(attend_kernel, n_chunk, shard_len),
-        out_shape=[cache, cache, jax.ShapeDtypeStruct((n_rows * batch, LANES), F32), jax.ShapeDtypeStruct((N_SEQ, 8, LANES), F32)],
-        in_specs=[SMEM, VMEM, ANY, ANY],
-        out_specs=[ANY, ANY, VMEM, VMEM],
+        out_shape=[cache, cache, pltpu.VMEM((n_rows * batch, LANES), F32), pltpu.VMEM((N_SEQ, 8, LANES), F32), held, held],
+        in_specs=[SMEM, VMEM, VMEM, VMEM],
+        out_specs=[HBM, HBM, VMEM, VMEM, VMEM, VMEM],
+        input_output_aliases={2: 4, 3: 5},
         scratch_shapes=[
-            pltpu.VMEM((batch, rows, LANES), BF16),
-            pltpu.VMEM((batch, rows, LANES), BF16),
             pltpu.VMEM((n_rows * batch, LANES), F32),
             pltpu.VMEM((N_SEQ * batch, LANES), F32),
             pltpu.SemaphoreType.DMA((2, n_chunk)),
-            pltpu.SemaphoreType.DMA((2, n_chunk)),
         ],
+        compiler_params=pltpu.CompilerParams(vmem_limit_bytes=6 * 2**20),
         name='attend',
     )(positions, qkv, k_cache, v_cache)
 
@@ -341,8 +355,8 @@
     dma = pltpu.SemaphoreType.DMA
     return pl.pallas_call(
         output_kernel,
-        out_shape=jax.ShapeDtypeStruct((batch, d_out), BF16),
-        in_specs=[VMEM, VMEM, ANY],
+        out_shape=pltpu.VMEM((batch, d_out), BF16),
+        in_specs=[VMEM, VMEM, HBM],
         out_specs=VMEM,
         scratch_shapes=[
             pltpu.VMEM((16, rows, width), BF16),
@@ -359,9 +373,9 @@
             dma((8,)), dma((8,)), dma((4,)), dma((4,)), dma((3,)), dma((3,)),
             dma((3,)), dma((3,)), dma((4,)), dma((4,)), dma((8,)), dma((8,)),
         ],
-        compiler_params=pltpu.CompilerParams(collective_id=1, has_side_effects=True),
+        compiler_params=pltpu.CompilerParams(collective_id=1, has_side_effects=True, vmem_limit_bytes=24 * 2**20),
         name='output',
-    )(mix.reshape(N_SEQ * n_q, batch, LANES), ml, w_out)
+    )(mix.reshape(N_SEQ * n_q, batch, LANES), ml, in_hbm(w_out))
 
 
 def solution(mesh):
@@ -370,8 +384,8 @@
     def local_step(tokens, w_query, w_key, w_value, w_out, k_cache, v_cache, positions):
         batch, shard_len, kv_local, head_dim = k_cache.shape
         flat = (batch, shard_len * kv_local, head_dim)
-        qkv = project(tokens, w_query, w_key, w_value)
-        k_new, v_new, mix, ml = attend(positions, qkv, k_cache.reshape(flat), v_cache.reshape(flat), shard_len)
+        qkv, k_held, v_held = project(tokens, w_query, w_key, w_value, k_cache.reshape(flat), v_cache.reshape(flat))
+        k_new, v_new, mix, ml, _, _ = attend(positions, qkv, k_held, v_held, shard_len)
         y = output(mix, ml, w_out)
         return y, k_new.reshape(k_cache.shape), v_new.reshape(v_cache.shape)
 

time: 81.8 us -> 75.6 us (0.924)
  Pallas kernels: 78.7 us -> 73.8 us
  local copies, waits for them, and re-layouts: 2.26 us -> 0.98 us
    pallas_call x1, Pallas kernels: 20.6 us -> 18.1 us  [attend(): pl.pallas_call(functools.partial(attend_kernel, n_chunk, shard_len), out_...]
    pallas_call x2, Pallas kernels: 58 us -> 55.7 us  [the longest x1 44 us: output(): pl.pallas_call(output_kernel, out_shape=pltpu.VMEM((batch, d_out), BF16),...]
    unnamed x1 -> x3, local copies, waits for them, and re-layouts: 2.26 us -> 0.98 us
where the time goes in v2:
time: 75.6 us; the launch traced here: 75.4 us
  Pallas kernels  73.8 us (98%)
  local copies, waits for them, and re-layouts  0.98 us (1%)
    pallas_call x1, Pallas kernels, output(): pl.pallas_call(output_kernel, out_shape=pltpu.VMEM((batch, d_out), BF16),...  44 us
    pallas_call x1, Pallas kernels, attend(): pl.pallas_call(functools.partial(attend_kernel, n_chunk, shard_len), out_...  18.1 us
    pallas_call x1, Pallas kernels, project(): pl.pallas_call(functools.partial(project_kernel, n_chunk, 4), out_shape=[...  11.7 us

profile of v2, /device:TPU:0, one launch (start us, length us, event | category | flops | bytes accessed | tf_op | source)
XLA Modules:
  0.0 75.4 jit_solution(12946545035948875852)
XLA Ops:
  0.6 0.0 copy-start
  0.6 11.7 %project.1 = (bf16[4,5,64,128]{3,2,1,0:T(8,128)(2,1)S(1)}, bf16[64,512,128]{2,1,0:T(8,128)(2,1)S(1)}, bf16[64,512,128]{2,1,0:T(8,128)(2,1)S(1)}) custom-call(bf16[64,8192]{1,0:T(8,128)(2,1)} %tok_hbm.1, bf16[8192,8192]{1,0:T(8,128)(2,1)} %wq_hbm.1, bf16[8192,1024]{1,0:T(8,128)(2,1)} %wk_hbm.1, bf16[8192,1024]{1,0:T(8,128)(2,1)} %wv_hbm.1, ...), custom_call_target="tpu_custom_call" | custom-call | tf_op jit(solution)/shard_map/project/pallas_call | solution.py:120
  12.4 0.0 copy-done
  12.4 18.1 %attend.1 = (bf16[64,512,128]{2,1,0:T(8,128)(2,1)}, bf16[64,512,128]{2,1,0:T(8,128)(2,1)}, f32[1024,128]{1,0:T(8,128)S(1)}, f32[4,8,128]{2,1,0:T(8,128)S(1)}, bf...) custom-call(s32[64]{0:T(128)S(1)} %copy-done, ...), custom_call_target="tpu_custom_call", output_to_operand_aliasing={{4}: (2, {}), {5}: (3, {})} | custom-call | tf_op jit(solution)/shard_map/attend/pallas_call | solution.py:211
  30.5 44.0 %output.1 = bf16[64,8192]{1,0:T(8,128)(2,1)S(1)} custom-call(f32[16,64,128]{2,1,0:T(8,128)S(1)} %bitcast.5, f32[4,8,128]{2,1,0:T(8,128)S(1)} %get-tuple-element.14.ml, bf16[512,8192]{1,0:T(8,128)(2,1)} %wo_hbm.1), custom_call_target="tpu_custom_call" | custom-call | tf_op jit(solution)/shard_map/output/pallas_call | solution.py:356
  74.4 1.0 %copy.16 = bf16[64,8192]{1,0:T(8,128)(2,1)} copy(bf16[64,8192]{1,0:T(8,128)(2,1)S(1)} %output.1) | data formatting | bytes 2097152
Async XLA Ops:
  0.6 11.8 %copy-start = (s32[64]{0:T(128)S(1)}, s32[64]{0:T(128)}, u32[]{:S(2)}) copy-start(s32[64]{0:T(128)} %pos_ref.1) | copy-start | bytes 772

commit v3 on v2

--- a/solution.py
+++ b/solution.py
@@ -170,27 +170,29 @@
             pos = pos_ref[b] - start
             inside = jnp.logical_and(pos >= 0, pos < shard_len)
             slot_at = jnp.clip(pos, 0, shard_len - 1)
-            base = pl.multiple_of((slot_at // 8) * 16, 16)
-            hit = win_slot == jnp.where(inside, lax.rem(slot_at, 8), -1)
+            base = pl.multiple_of((slot_at >> 3) * 16, 16)
+            hit = win_slot == jnp.where(inside, slot_at & 7, -1)
             for buf, first in ((kbuf, 0), (vbuf, 2)):
                 new = jnp.where(win_odd, kvf[pl.ds((first + 1) * batch + b, 1), :], kvf[pl.ds(first * batch + b, 1), :])
                 old = buf[b, pl.ds(base, 16), :]
                 buf[b, pl.ds(base, 16), :] = jnp.where(hit, new.astype(BF16), old)
         store(k_out, kbuf, 0, c).start()
         store(v_out, vbuf, 1, c).start()
-        for j in range(per):
-            b = c * per + j
-            limit = pos_ref[b] - start
+        index = [c * per + j for j in range(per)]
+        scores = []
+        for b in index:
             q = qf[pl.ds(b, n_rows, stride=batch), :].astype(BF16)
-            s = lax.dot_general(q, kbuf[b], (((1,), (1,)), ((), ())), preferred_element_type=F32) * LANES ** -0.5
-            s = jnp.where(slot <= limit, s, -jnp.inf)
+            scores.append(lax.dot_general(q, kbuf[b], (((1,), (1,)), ((), ())), preferred_element_type=F32))
+        weights = []
+        for b, s in zip(index, scores):
+            s = jnp.where(slot <= pos_ref[b] - start, s * LANES ** -0.5, -jnp.inf)
             m = jnp.max(s, axis=1, keepdims=True)
-            safe = jnp.where(m == -jnp.inf, 0.0, m)
-            w = jnp.exp(s - safe)
+            w = jnp.exp(s - jnp.where(m == -jnp.inf, 0.0, m))
             l = jnp.sum(w, axis=1, keepdims=True)
-            mix = jnp.dot(w.astype(BF16), vbuf[b], preferred_element_type=F32)
-            mix_out[pl.ds(b, n_rows, stride=batch), :] = mix
+            weights.append(w.astype(BF16))
             ml = jnp.where(lane == b, m, jnp.where(lane == batch + b, l, ml))
+        for b, w in zip(index, weights):
+            mix_out[pl.ds(b, n_rows, stride=batch), :] = jnp.dot(w, vbuf[b], preferred_element_type=F32)
         return ml
 
     ml = lax.fori_loop(0, n_chunk, chunk, jnp.zeros((n_rows, LANES), F32))
@@ -205,7 +207,7 @@
 def attend(positions, qkv, k_cache, v_cache, shard_len):
     batch, rows, _ = k_cache.shape
     n_rows = N_SEQ * (qkv.shape[1] - 1)
-    n_chunk = 8
+    n_chunk = 4
     cache = pltpu.HBM(k_cache.shape, BF16)
     held = pltpu.VMEM(k_cache.shape, BF16)
     return pl.pallas_call(

time: 75.6 us -> 65 us (0.86)
  Pallas kernels: 73.8 us -> 63.2 us
    pallas_call x1, Pallas kernels: 18.1 us -> 7.47 us  [attend(): pl.pallas_call(functools.partial(attend_kernel, n_chunk, shard_len), out_...]
where the time goes in v3:
time: 65 us; the launch traced here: 64.8 us
  Pallas kernels  63.2 us (97%)
  local copies, waits for them, and re-layouts  0.98 us (2%)
  between operations  0.67 us (1%)
    pallas_call x1, Pallas kernels, output(): pl.pallas_call(output_kernel, out_shape=pltpu.VMEM((batch, d_out), BF16),...  44 us
    pallas_call x1, Pallas kernels, project(): pl.pallas_call(functools.partial(project_kernel, n_chunk, 4), out_shape=[...  11.7 us
    pallas_call x1, Pallas kernels, attend(): pl.pallas_call(functools.partial(attend_kernel, n_chunk, shard_len), out_...  7.47 us

profile of v3, /device:TPU:0, one launch (start us, length us, event | category | flops | bytes accessed | tf_op | source)
XLA Modules:
  0.0 64.8 jit_solution(10210150222811740553)
XLA Ops:
  0.6 0.0 copy-start
  0.6 11.7 %project.1 = (bf16[4,5,64,128]{3,2,1,0:T(8,128)(2,1)S(1)}, bf16[64,512,128]{2,1,0:T(8,128)(2,1)S(1)}, bf16[64,512,128]{2,1,0:T(8,128)(2,1)S(1)}) custom-call(bf16[64,8192]{1,0:T(8,128)(2,1)} %tok_hbm.1, bf16[8192,8192]{1,0:T(8,128)(2,1)} %wq_hbm.1, bf16[8192,1024]{1,0:T(8,128)(2,1)} %wk_hbm.1, bf16[8192,1024]{1,0:T(8,128)(2,1)} %wv_hbm.1, ...), custom_call_target="tpu_custom_call" | custom-call | tf_op jit(solution)/shard_map/project/pallas_call | solution.py:120
  12.4 0.0 copy-done
  12.4 7.5 %attend.1 = (bf16[64,512,128]{2,1,0:T(8,128)(2,1)}, bf16[64,512,128]{2,1,0:T(8,128)(2,1)}, f32[1024,128]{1,0:T(8,128)S(1)}, f32[4,8,128]{2,1,0:T(8,128)S(1)}, bf...) custom-call(s32[64]{0:T(128)S(1)} %copy-done, ...), custom_call_target="tpu_custom_call", output_to_operand_aliasing={{4}: (2, {}), {5}: (3, {})} | custom-call | tf_op jit(solution)/shard_map/attend/pallas_call | solution.py:213
  19.9 44.0 %output.1 = bf16[64,8192]{1,0:T(8,128)(2,1)S(1)} custom-call(f32[16,64,128]{2,1,0:T(8,128)S(1)} %bitcast.5, f32[4,8,128]{2,1,0:T(8,128)S(1)} %get-tuple-element.14.ml, bf16[512,8192]{1,0:T(8,128)(2,1)} %wo_hbm.1), custom_call_target="tpu_custom_call" | custom-call | tf_op jit(solution)/shard_map/output/pallas_call | solution.py:358
  63.8 1.0 %copy.16 = bf16[64,8192]{1,0:T(8,128)(2,1)} copy(bf16[64,8192]{1,0:T(8,128)(2,1)S(1)} %output.1) | data formatting | bytes 2097152
Async XLA Ops:
  0.6 11.8 %copy-start = (s32[64]{0:T(128)S(1)}, s32[64]{0:T(128)}, u32[]{:S(2)}) copy-start(s32[64]{0:T(128)} %pos_ref.1) | copy-start | bytes 772

commit v4 on v3

v4 whole, which is shorter than its diff:
```python
import functools

import jax
import jax.numpy as jnp
from jax import lax
from jax.experimental import pallas as pl
from jax.experimental.pallas import tpu as pltpu
from jax.sharding import PartitionSpec as P

MESH = pl.DeviceIdType.MESH
HBM = pl.BlockSpec(memory_space=pltpu.HBM)
VMEM = pl.BlockSpec(memory_space=pltpu.VMEM)
SMEM = pl.BlockSpec(memory_space=pltpu.SMEM)
N_SEQ = 4
N_HEAD = 4
LANES = 128
F32 = jnp.float32
BF16 = jnp.bfloat16


def in_hbm(x):
    return pltpu.with_memory_space_constraint(x, pltpu.HBM)


def entry_barrier(axes):
    sem = pltpu.get_barrier_semaphore()
    count = 0
    for axis, size in axes:
        me = lax.axis_index(axis)
        for step in range(1, size):
            pl.semaphore_signal(sem, inc=1, device_id={axis: lax.rem(me + step, size)}, device_id_type=MESH)
            count += 1
    return lambda: pl.semaphore_wait(sem, count)


def project_kernel(n_chunk, ahead, tok_hbm, wq_hbm, wk_hbm, wv_hbm, k_hbm, v_hbm, out, kbuf, vbuf, tok, w_first, w_second,
                   acc_first, acc_second, stage, load_sem, cache_sem, send_sem, recv_sem):
    head, seq = lax.axis_index('head'), lax.axis_index('seq')
    depth = w_first.shape[1]
    batch = tok.shape[0]
    wait_peers = entry_barrier((('seq', N_SEQ),))

    second = w_second.shape[2]
    first = w_first.shape[2] - LANES
    q_at = (head * N_SEQ + seq) * (first + second)
    kv_at = pl.multiple_of((head * 2 + lax.rem(seq, 2)) * LANES, LANES)

    def tok_copy(c):
        return pltpu.make_async_copy(tok_hbm.at[:, pl.ds(c * depth, depth)], tok.at[:, pl.ds(c * depth, depth)], load_sem.at[0, c])

    def kv_copy(src, c):
        return pltpu.make_async_copy(src.at[pl.ds(c * depth, depth), pl.ds(kv_at, LANES)], w_first.at[c, :, pl.ds(0, LANES)],
                                     load_sem.at[1, c])

    def q_copy(r, c):
        rows = pl.ds(c * depth, depth)
        if r == 0:
            at = pl.multiple_of(q_at, LANES)
            return pltpu.make_async_copy(wq_hbm.at[rows, pl.ds(at, first)], w_first.at[c, :, pl.ds(LANES, first)], load_sem.at[2, c])
        at = pl.multiple_of(q_at + first, LANES)
        return pltpu.make_async_copy(wq_hbm.at[rows, pl.ds(at, second)], w_second.at[c], load_sem.at[3, c])

    def start(r, c):
        q_copy(r, c).start()
        if r == 0:
            tok_copy(c).start()

            @pl.when(seq < 2)
            def _():
                kv_copy(wk_hbm, c).start()

            @pl.when(seq >= 2)
            def _():
                kv_copy(wv_hbm, c).start()

    caches = []
    for g in range(8):
        span = pl.ds(g * (batch // 8), batch // 8)
        caches.append(pltpu.make_async_copy(k_hbm.at[span], kbuf.at[span], cache_sem.at[0, g]))
        caches.append(pltpu.make_async_copy(v_hbm.at[span], vbuf.at[span], cache_sem.at[1, g]))
    share = len(caches) // ahead
    held = 0

    turns = [(r, c) for r in range(2) for c in range(n_chunk)]
    copies = []
    for r, c in turns[:ahead]:
        start(r, c)
    for n, (r, c) in enumerate(turns):
        if n + ahead < len(turns):
            start(*turns[n + ahead])
        else:
            for copy in caches[held:held + share]:
                copy.start()
            held += share
        q_copy(r, c).wait()
        if r == 0:
            tok_copy(c).wait()
            kv_copy(wk_hbm, c).wait()
        acc, w = ((acc_first, w_first), (acc_second, w_second))[r]
        part = jnp.dot(tok[:, c * depth:(c + 1) * depth], w[c], preferred_element_type=F32)
        if c == 0:
            acc[...] = part
        else:
            acc[...] += part
        if c == n_chunk - 1:
            at, count = (0, acc.shape[1] // LANES) if r == 0 else (w_first.shape[2] // LANES, acc.shape[1] // LANES)
            for i in range(count):
                stage[at + i] = acc[:, i * LANES:(i + 1) * LANES].astype(BF16)
            if r == 0:
                wait_peers()
            for step in (2, 1, 3):
                copies.append(pltpu.make_async_remote_copy(
                    src_ref=stage.at[pl.ds(at, count)], dst_ref=out.at[seq, pl.ds(at, count)],
                    send_sem=send_sem.at[r, step - 1], recv_sem=recv_sem.at[r, step - 1],
                    device_id={'seq': lax.rem(seq + step, N_SEQ)}, device_id_type=MESH))
                copies[-1].start()
            out[seq, at:at + count] = stage[at:at + count]
    for copy in copies:
        copy.wait()
    for copy in caches:
        copy.wait()


def project(tokens, w_query, w_key, w_value, k_cache, v_cache):
    batch, d_model = tokens.shape
    q_cols = w_query.shape[1] // (N_HEAD * N_SEQ)
    n_chunk = 8
    depth = d_model // n_chunk
    n_q = q_cols // LANES
    first = LANES + q_cols // 2
    second = q_cols - q_cols // 2
    return pl.pallas_call(
        functools.partial(project_kernel, n_chunk, 8),
        out_shape=[pltpu.VMEM((N_SEQ, n_q + 1, batch, LANES), BF16), pltpu.VMEM(k_cache.shape, BF16), pltpu.VMEM(k_cache.shape, BF16)],
        in_specs=[HBM] * 6,
        out_specs=[VMEM] * 3,
        scratch_shapes=[
            pltpu.VMEM((batch, d_model), BF16),
            pltpu.VMEM((n_chunk, depth, first), BF16),
            pltpu.VMEM((n_chunk, depth, second), BF16),
            pltpu.VMEM((batch, first), F32),
            pltpu.VMEM((batch, second), F32),
            pltpu.VMEM((n_q + 1, batch, LANES), BF16),
            pltpu.SemaphoreType.DMA((4, n_chunk)),
            pltpu.SemaphoreType.DMA((2, 8)),
            pltpu.SemaphoreType.DMA((2, N_SEQ - 1)),
            pltpu.SemaphoreType.DMA((2, N_SEQ - 1)),
        ],
        compiler_params=pltpu.CompilerParams(collective_id=0, has_side_effects=True, vmem_limit_bytes=18 * 2**20),
        name='project',
    )(*map(in_hbm, (tokens, w_query, w_key, w_value, k_cache, v_cache)))


def attend_kernel(n_chunk, shard_len, pos_ref, qkv_ref, k_in, v_in, k_out, v_out, mix_out, ml_out, kbuf, vbuf,
                  qf, kvf, store_sem):
    batch, rows = kbuf.shape[0], kbuf.shape[1]
    n_q = qkv_ref.shape[1] - 1
    n_rows = N_SEQ * n_q
    per = batch // n_chunk
    start = lax.axis_index('seq') * shard_len

    def store(hbm, buf, which, c):
        return pltpu.make_async_copy(buf.at[pl.ds(c * per, per)], hbm.at[pl.ds(c * per, per)], store_sem.at[which, c])

    for s in range(N_SEQ):
        for i in range(n_q):
            at = (s * n_q + i) * batch
            qf[at:at + batch, :] = qkv_ref[s, 1 + i].astype(F32)
        kvf[s * batch:(s + 1) * batch, :] = qkv_ref[s, 0].astype(F32)

    col = lax.broadcasted_iota(jnp.int32, (n_rows, rows), 1)
    row = lax.broadcasted_iota(jnp.int32, (n_rows, rows), 0)
    slot = jnp.where((col & 1) == row // (n_rows // 2), col >> 1, jnp.int32(1 << 30))
    win_row = lax.broadcasted_iota(jnp.int32, (16, LANES), 0)
    win_odd = (win_row & 1) == 1
    win_slot = win_row >> 1
    lane = lax.broadcasted_iota(jnp.int32, (n_rows, LANES), 1)

    def chunk(c, ml):
        for j in range(per):
            b = c * per + j
            pos = pos_ref[b] - start
            inside = jnp.logical_and(pos >= 0, pos < shard_len)
            slot_at = jnp.clip(pos, 0, shard_len - 1)
            base = pl.multiple_of((slot_at >> 3) * 16, 16)
            hit = win_slot == jnp.where(inside, slot_at & 7, -1)
            for buf, first in ((kbuf, 0), (vbuf, 2)):
                new = jnp.where(win_odd, kvf[pl.ds((first + 1) * batch + b, 1), :], kvf[pl.ds(first * batch + b, 1), :])
                old = buf[b, pl.ds(base, 16), :]
                buf[b, pl.ds(base, 16), :] = jnp.where(hit, new.astype(BF16), old)
        store(k_out, kbuf, 0, c).start()
        store(v_out, vbuf, 1, c).start()
        index = [c * per + j for j in range(per)]
        scores = []
        for b in index:
            q = qf[pl.ds(b, n_rows, stride=batch), :].astype(BF16)
            scores.append(lax.dot_general(q, kbuf[b], (((1,), (1,)), ((), ())), preferred_element_type=F32))
        weights = []
        for b, s in zip(index, scores):
            s = jnp.where(slot <= pos_ref[b] - start, s * LANES ** -0.5, -jnp.inf)
            m = jnp.max(s, axis=1, keepdims=True)
            w = jnp.exp(s - jnp.where(m == -jnp.inf, 0.0, m))
            l = jnp.sum(w, axis=1, keepdims=True)
            weights.append(w.astype(BF16))
            ml = jnp.where(lane == b, m, jnp.where(lane == batch + b, l, ml))
        for b, w in zip(index, weights):
            mix_out[pl.ds(b, n_rows, stride=batch), :] = jnp.dot(w, vbuf[b], preferred_element_type=F32)
        return ml

    ml = lax.fori_loop(0, n_chunk, chunk, jnp.zeros((n_rows, LANES), F32))
    ml_out[...] = jnp.zeros_like(ml_out)
    for s in range(N_SEQ):
        ml_out[s, 0:n_q, :] = ml[s * n_q:(s + 1) * n_q, :]
    for c in range(n_chunk):
        store(k_out, kbuf, 0, c).wait()
        store(v_out, vbuf, 1, c).wait()


def attend(positions, qkv, k_cache, v_cache, shard_len):
    batch, rows, _ = k_cache.shape
    n_rows = N_SEQ * (qkv.shape[1] - 1)
    n_chunk = 4
    cache = pltpu.HBM(k_cache.shape, BF16)
    held = pltpu.VMEM(k_cache.shape, BF16)
    return pl.pallas_call(
        functools.partial(attend_kernel, n_chunk, shard_len),
        out_shape=[cache, cache, pltpu.VMEM((n_rows * batch, LANES), F32), pltpu.VMEM((N_SEQ, 8, LANES), F32), held, held],
        in_specs=[SMEM, VMEM, VMEM, VMEM],
        out_specs=[HBM, HBM, VMEM, VMEM, VMEM, VMEM],
        input_output_aliases={2: 4, 3: 5},
        scratch_shapes=[
            pltpu.VMEM((n_rows * batch, LANES), F32),
            pltpu.VMEM((N_SEQ * batch, LANES), F32),
            pltpu.SemaphoreType.DMA((2, n_chunk)),
        ],
        compiler_params=pltpu.CompilerParams(vmem_limit_bytes=6 * 2**20),
        name='attend',
    )(positions, qkv, k_cache, v_cache)


def lane_table(rows):
    fill = jnp.zeros((LANES - 8 * len(rows), LANES), F32)
    return jnp.concatenate(list(rows) + [fill], axis=0).T


def merge(parts, batch):
    top = functools.reduce(jnp.maximum, parts)
    safe = jnp.where(top == -jnp.inf, 0.0, top)
    factors = [jnp.exp(p - safe) for p in parts]
    total = functools.reduce(jnp.add, [pltpu.roll(p, LANES - batch, 1) * e for p, e in zip(parts, factors)])
    return top, total, factors


def output_kernel(n_pass, mix, ml, wo_hbm, y, wo, pair_in, far_in, pair_ml, far_ml, far_give, far_give_ml, attn, give, own, core_in, y_in, z_in,
                  wo_sem, p_send, p_recv, f_send, f_recv, c_send, c_recv, y_send, y_recv, z_send, z_recv,
                  gz_send, gz_recv, gy_send, gy_recv, gc_send, gc_recv):
    head, seq = lax.axis_index('head'), lax.axis_index('seq')
    side, core = seq // 2, lax.rem(seq, 2)
    partner = side * 2 + (1 - core)
    across = (1 - side) * 2 + core
    diagonal = (1 - side) * 2 + (1 - core)
    n_q, batch = pair_in.shape[1], pair_in.shape[2]
    narrow = z_in.shape[3]
    wait_peers = entry_barrier((('seq', N_SEQ), ('head', N_HEAD)))

    def column(half, quarter, z, p):
        return pl.multiple_of((((half * 2 + quarter) * N_HEAD + z) * n_pass + p) * narrow, narrow)

    def unit(mine, near, p):
        return ((1 if mine else 0) * 2 + (1 if near else 0)) * n_pass + p

    def wo_copy(mine, near, p, j):
        at = column(core if mine else 1 - core, side if near else 1 - side, lax.rem(head + j, N_HEAD), p)
        u = unit(mine, near, p)
        return pltpu.make_async_copy(wo_hbm.at[:, pl.ds(at, narrow)], wo.at[u, :, pl.ds(j * narrow, narrow)], wo_sem.at[u, j])

    order = [(mine, near, p) for near in (False, True) for mine in (False, True) for p in range(n_pass)]
    for mine, near, p in order:
        for j in range(N_HEAD):
            wo_copy(mine, near, p, j).start()

    def remote(src, dst, send, recv, device):
        copy = pltpu.make_async_remote_copy(src_ref=src, dst_ref=dst, send_sem=send, recv_sem=recv, device_id=device, device_id_type=MESH)
        copy.start()
        return copy

    wait_peers()
    pair = []
    for n, to in enumerate((diagonal, partner)):
        pair.append(remote(ml.at[to], pair_ml.at[n], p_send.at[0, n], p_recv.at[0, n], {'seq': partner}))
        pair.append(remote(mix.at[pl.ds(to * n_q, n_q)], pair_in.at[n], p_send.at[1, n], p_recv.at[1, n], {'seq': partner}))
    pair[0].wait_recv()
    pair[1].wait_recv()
    top, total, factors = merge([ml[across], pair_ml[0]], batch)
    lane = lax.broadcasted_iota(jnp.int32, (8, LANES), 1)
    far_give_ml[...] = jnp.where(lane < batch, top, pltpu.roll(total, batch, 1))
    table = lane_table(factors)
    for i in range(n_q):
        far_give[i] = mix[across * n_q + i] * table[0:batch, i:i + 1] + pair_in[0, i] * table[0:batch, 8 + i:9 + i]
    far = [remote(far_give_ml, far_ml, f_send.at[0], f_recv.at[0], {'seq': across}),
           remote(far_give, far_in, f_send.at[1], f_recv.at[1], {'seq': across})]
    pair[2].wait_recv()
    pair[3].wait_recv()
    for copy in far:
        copy.wait_recv()
    _, total, factors = merge([ml[seq], pair_ml[1], far_ml[...]], batch)
    table = lane_table([e / total for e in factors])
    for i in range(n_q):
        value = mix[seq * n_q + i] * table[0:batch, i:i + 1]
        value += pair_in[1, i] * table[0:batch, 8 + i:9 + i]
        value += far_in[i] * table[0:batch, 16 + i:17 + i]
        attn[:, i * LANES:(i + 1) * LANES] = value.astype(BF16)
    sends = pair + far

    for mine, near, p in order:
        for j in range(N_HEAD):
            wo_copy(mine, near, p, j).wait()

    def partial(mine, near, p):
        return jnp.dot(attn[...], wo[unit(mine, near, p)], preferred_element_type=F32)

    def hand(near, p):
        u = unit(False, near, p)
        give[u] = partial(False, near, p)
        c_copies[near, p] = remote(give.at[u], core_in.at[u], c_send.at[u], c_recv.at[u], {'seq': partner})

    def keep(near, p):
        u = unit(False, near, p)
        value = partial(True, near, p)
        c_copies[near, p].wait_recv()
        own[u] = value + core_in[u]

    c_copies, y_copies, z_copies = {}, {}, {}
    for p in range(n_pass):
        hand(False, p)
    for p in range(n_pass):
        keep(False, p)
        y_copies[p] = remote(own.at[unit(False, False, p)], y_in.at[p], y_send.at[p], y_recv.at[p], {'seq': across})
    for p in range(n_pass):
        hand(True, p)
    for p in range(n_pass):
        keep(True, p)

    def along(p):
        u = unit(False, True, p)
        y_copies[p].wait_recv()
        own[u] = own[u] + y_in[p]
        for step in (2, 1, 3):
            z_copies[p, step] = remote(own.at[u, :, pl.ds(step * narrow, narrow)], z_in.at[p, step - 1], z_send.at[p, step - 1],
                                       z_recv.at[p, step - 1], {'head': lax.rem(head + step, N_HEAD)})

    def spread(half, quarter, z, p, send, recv, device):
        at = y.at[:, pl.ds(column(half, quarter, z, p), narrow)]
        return remote(at, at, send, recv, device)

    gz, gy, gc = {}, {}, {}

    def fan(z, p, step):
        gy[p, step] = spread(core, side, z, p, gy_send.at[p, step], gy_recv.at[p, step], {'seq': across})
        gc[p, step] = spread(core, side, z, p, gc_send.at[p, step], gc_recv.at[p, step], {'seq': partner})

    def finish(p):
        for step in (1, 3, 2):
            z_copies[p, step].wait_recv()
        value = own[unit(False, True, p), :, 0:narrow] + z_in[p, 0] + z_in[p, 1] + z_in[p, 2]
        y[:, pl.ds(column(core, side, head, p), narrow)] = value.astype(BF16)
        for step in (2, 1, 3):
            gz[p, step] = spread(core, side, head, p, gz_send.at[p, step - 1], gz_recv.at[p, step - 1], {'head': lax.rem(head + step, N_HEAD)})
        fan(head, p, 0)

    def over(p):
        for step in (1, 3, 2):
            gz[p, step].wait_recv()
            fan(lax.rem(head + N_HEAD - step, N_HEAD), p, step)

    def to_partner(p):
        for step in (0, 1, 3, 2):
            gy[p, step].wait_recv()
            z = lax.rem(head + N_HEAD - step, N_HEAD)
            gc[p, 4 + step] = spread(core, 1 - side, z, p, gc_send.at[p, 4 + step], gc_recv.at[p, 4 + step], {'seq': partner})

    stages = [(3 * p + at, n, p) for n, at in enumerate((0, 4.6, 9.3, 11.4)) for p in range(n_pass)]
    for _, n, p in sorted(stages):
        (along, finish, over, to_partner)[n](p)
    for copy in gc.values():
        copy.wait_recv()
    for group in (sends, *(g.values() for g in (c_copies, y_copies, z_copies, gz, gy, gc))):
        for copy in group:
            copy.wait_send()


def output(mix, ml, w_out):
    rows, d_out = w_out.shape
    n_q = rows // LANES
    batch = mix.shape[0] // (N_SEQ * n_q)
    n_pass = 4
    width = d_out // 16
    narrow = width // n_pass
    dma = pltpu.SemaphoreType.DMA
    block = pltpu.VMEM((n_q, batch, LANES), F32)
    return pl.pallas_call(
        functools.partial(output_kernel, n_pass),
        out_shape=pltpu.VMEM((batch, d_out), BF16),
        in_specs=[VMEM, VMEM, HBM],
        out_specs=VMEM,
        scratch_shapes=[
            pltpu.VMEM((4 * n_pass, rows, N_HEAD * narrow), BF16),
            pltpu.VMEM((2, n_q, batch, LANES), F32),
            block,
            pltpu.VMEM((2, 8, LANES), F32),
            pltpu.VMEM((8, LANES), F32),
            block,
            pltpu.VMEM((8, LANES), F32),
            pltpu.VMEM((batch, rows), BF16),
            pltpu.VMEM((2 * n_pass, batch, width), F32),
            pltpu.VMEM((2 * n_pass, batch, width), F32),
            pltpu.VMEM((2 * n_pass, batch, width), F32),
            pltpu.VMEM((n_pass, batch, width), F32),
            pltpu.VMEM((n_pass, 3, batch, narrow), F32),
            dma((4 * n_pass, N_HEAD)),
            dma((2, 2)), dma((2, 2)), dma((2,)), dma((2,)),
            dma((2 * n_pass,)), dma((2 * n_pass,)), dma((n_pass,)), dma((n_pass,)), dma((n_pass, 3)), dma((n_pass, 3)),
            dma((n_pass, 3)), dma((n_pass, 3)), dma((n_pass, 4)), dma((n_pass, 4)), dma((n_pass, 8)), dma((n_pass, 8)),
        ],
        compiler_params=pltpu.CompilerParams(collective_id=1, has_side_effects=True, vmem_limit_bytes=24 * 2**20),
        name='output',
    )(mix.reshape(N_SEQ * n_q, batch, LANES), ml, in_hbm(w_out))


def solution(mesh):
    cache_spec = P('rep', 'seq', 'head', None)

    def local_step(tokens, w_query, w_key, w_value, w_out, k_cache, v_cache, positions):
        batch, shard_len, kv_local, head_dim = k_cache.shape
        flat = (batch, shard_len * kv_local, head_dim)
        qkv, k_held, v_held = project(tokens, w_query, w_key, w_value, k_cache.reshape(flat), v_cache.reshape(flat))
        k_new, v_new, mix, ml, _, _ = attend(positions, qkv, k_held, v_held, shard_len)
        y = output(mix, ml, w_out)
        return y, k_new.reshape(k_cache.shape), v_new.reshape(v_cache.shape)

    return jax.shard_map(
        local_step,
        mesh=mesh,
        in_specs=(P('rep', None), P(), P(), P(), P(('head', 'seq'), None), cache_spec, cache_spec, P('rep')),
        out_specs=(P('rep', None), cache_spec, cache_spec),
        check_vma=False,
    )
```

time: 65 us -> 65.1 us (level)
  no operation moved by 1% of the time
where the time goes in v4:
time: 65.1 us; the launch traced here: 64.9 us
  Pallas kernels  63.3 us (97%)
  local copies, waits for them, and re-layouts  0.98 us (2%)
  between operations  0.67 us (1%)
    pallas_call x1, Pallas kernels, output(): pl.pallas_call(functools.partial(output_kernel, n_pass), out_shape=pltpu....  44.9 us
    pallas_call x1, Pallas kernels, project(): pl.pallas_call(functools.partial(project_kernel, n_chunk, 8), out_shape=[...  11 us
    pallas_call x1, Pallas kernels, attend(): pl.pallas_call(functools.partial(attend_kernel, n_chunk, shard_len), out_...  7.47 us

profile of v4, /device:TPU:0, one launch (start us, length us, event | category | flops | bytes accessed | tf_op | source)
XLA Modules:
  0.0 64.9 jit_solution(13847809472144341729)
XLA Ops:
  0.6 0.0 copy-start
  0.6 11.0 %project.1 = (bf16[4,5,64,128]{3,2,1,0:T(8,128)(2,1)S(1)}, bf16[64,512,128]{2,1,0:T(8,128)(2,1)S(1)}, bf16[64,512,128]{2,1,0:T(8,128)(2,1)S(1)}) custom-call(bf16[64,8192]{1,0:T(8,128)(2,1)} %tok_hbm.1, bf16[8192,8192]{1,0:T(8,128)(2,1)} %wq_hbm.1, bf16[8192,1024]{1,0:T(8,128)(2,1)} %wk_hbm.1, bf16[8192,1024]{1,0:T(8,128)(2,1)} %wv_hbm.1, ...), custom_call_target="tpu_custom_call" | custom-call | tf_op jit(solution)/shard_map/project/pallas_call | solution.py:132
  11.6 0.0 copy-done
  11.6 7.5 %attend.1 = (bf16[64,512,128]{2,1,0:T(8,128)(2,1)}, bf16[64,512,128]{2,1,0:T(8,128)(2,1)}, f32[1024,128]{1,0:T(8,128)S(1)}, f32[4,8,128]{2,1,0:T(8,128)S(1)}, bf...) custom-call(s32[64]{0:T(128)S(1)} %copy-done, ...), custom_call_target="tpu_custom_call", output_to_operand_aliasing={{4}: (2, {}), {5}: (3, {})} | custom-call | tf_op jit(solution)/shard_map/attend/pallas_call | solution.py:225
  19.1 44.9 %output.1 = bf16[64,8192]{1,0:T(8,128)(2,1)S(1)} custom-call(f32[16,64,128]{2,1,0:T(8,128)S(1)} %bitcast.5, f32[4,8,128]{2,1,0:T(8,128)S(1)} %get-tuple-element.14.ml, bf16[512,8192]{1,0:T(8,128)(2,1)} %wo_hbm.1), custom_call_target="tpu_custom_call" | custom-call | tf_op jit(solution)/shard_map/output/pallas_call | solution.py:401
  64.0 1.0 %copy.16 = bf16[64,8192]{1,0:T(8,128)(2,1)} copy(bf16[64,8192]{1,0:T(8,128)(2,1)S(1)} %output.1) | data formatting | bytes 2097152
Async XLA Ops:
  0.6 11.0 %copy-start = (s32[64]{0:T(128)S(1)}, s32[64]{0:T(128)}, u32[]{:S(2)}) copy-start(s32[64]{0:T(128)} %pos_ref.1) | copy-start | bytes 772

commit v5 on v4

--- a/solution.py
+++ b/solution.py
@@ -263,21 +263,21 @@
     narrow = z_in.shape[3]
     wait_peers = entry_barrier((('seq', N_SEQ), ('head', N_HEAD)))
 
-    def column(half, quarter, z, p):
-        return pl.multiple_of((((half * 2 + quarter) * N_HEAD + z) * n_pass + p) * narrow, narrow)
-
-    def unit(mine, near, p):
-        return ((1 if mine else 0) * 2 + (1 if near else 0)) * n_pass + p
-
-    def wo_copy(mine, near, p, j):
-        at = column(core if mine else 1 - core, side if near else 1 - side, lax.rem(head + j, N_HEAD), p)
-        u = unit(mine, near, p)
-        return pltpu.make_async_copy(wo_hbm.at[:, pl.ds(at, narrow)], wo.at[u, :, pl.ds(j * narrow, narrow)], wo_sem.at[u, j])
-
-    order = [(mine, near, p) for near in (False, True) for mine in (False, True) for p in range(n_pass)]
-    for mine, near, p in order:
-        for j in range(N_HEAD):
-            wo_copy(mine, near, p, j).start()
+    def column(half, quarter, p, z=None):
+        at = ((half * 2 + quarter) * n_pass + p) * N_HEAD * narrow
+        return pl.multiple_of(at if z is None else at + z * narrow, narrow)
+
+    def strip(z):
+        return pl.ds(pl.multiple_of(z * narrow, narrow), narrow)
+
+    def unit(near, p):
+        return (1 if near else 0) * n_pass + p
+
+    n_part = wo_sem.shape[0]
+    part = wo.shape[0] // n_part
+    wo_copies = [pltpu.make_async_copy(wo_hbm.at[pl.ds(n * part, part)], wo.at[pl.ds(n * part, part)], wo_sem.at[n]) for n in range(n_part)]
+    for copy in wo_copies:
+        copy.start()
 
     def remote(src, dst, send, recv, device):
         copy = pltpu.make_async_remote_copy(src_ref=src, dst_ref=dst, send_sem=send, recv_sem=recv, device_id=device, device_id_type=MESH)
@@ -312,22 +312,22 @@
         attn[:, i * LANES:(i + 1) * LANES] = value.astype(BF16)
     sends = pair + far
 
-    for mine, near, p in order:
-        for j in range(N_HEAD):
-            wo_copy(mine, near, p, j).wait()
-
-    def partial(mine, near, p):
-        return jnp.dot(attn[...], wo[unit(mine, near, p)], preferred_element_type=F32)
+    for copy in wo_copies:
+        copy.wait()
+
+    def partial(half, near, p):
+        at = column(half, side if near else 1 - side, p)
+        return jnp.dot(attn[...], wo[:, pl.ds(at, N_HEAD * narrow)], preferred_element_type=F32)
 
     def hand(near, p):
-        u = unit(False, near, p)
-        give[u] = partial(False, near, p)
-        c_copies[near, p] = remote(give.at[u], core_in.at[u], c_send.at[u], c_recv.at[u], {'seq': partner})
+        u = unit(near, p)
+        give[u] = partial(1 - core, near, p)
+        c_copies[u] = remote(give.at[u], core_in.at[u], c_send.at[u], c_recv.at[u], {'seq': partner})
 
     def keep(near, p):
-        u = unit(False, near, p)
-        value = partial(True, near, p)
-        c_copies[near, p].wait_recv()
+        u = unit(near, p)
+        value = partial(core, near, p)
+        c_copies[u].wait_recv()
         own[u] = value + core_in[u]
 
     c_copies, y_copies, z_copies = {}, {}, {}
@@ -335,49 +335,44 @@
         hand(False, p)
     for p in range(n_pass):
         keep(False, p)
-        y_copies[p] = remote(own.at[unit(False, False, p)], y_in.at[p], y_send.at[p], y_recv.at[p], {'seq': across})
+        y_copies[p] = remote(own.at[unit(False, p)], y_in.at[p], y_send.at[p], y_recv.at[p], {'seq': across})
     for p in range(n_pass):
         hand(True, p)
     for p in range(n_pass):
         keep(True, p)
 
     def along(p):
-        u = unit(False, True, p)
+        u = unit(True, p)
         y_copies[p].wait_recv()
         own[u] = own[u] + y_in[p]
         for step in (2, 1, 3):
-            z_copies[p, step] = remote(own.at[u, :, pl.ds(step * narrow, narrow)], z_in.at[p, step - 1], z_send.at[p, step - 1],
-                                       z_recv.at[p, step - 1], {'head': lax.rem(head + step, N_HEAD)})
-
-    def spread(half, quarter, z, p, send, recv, device):
-        at = y.at[:, pl.ds(column(half, quarter, z, p), narrow)]
+            to = lax.rem(head + step, N_HEAD)
+            z_copies[p, step] = remote(own.at[u, :, strip(to)], z_in.at[p, step - 1], z_send.at[p, step - 1], z_recv.at[p, step - 1],
+                                       {'head': to})
+
+    def spread(half, quarter, p, z, send, recv, device):
+        at = y.at[:, pl.ds(column(half, quarter, p, z), narrow if z is not None else N_HEAD * narrow)]
         return remote(at, at, send, recv, device)
 
     gz, gy, gc = {}, {}, {}
-
-    def fan(z, p, step):
-        gy[p, step] = spread(core, side, z, p, gy_send.at[p, step], gy_recv.at[p, step], {'seq': across})
-        gc[p, step] = spread(core, side, z, p, gc_send.at[p, step], gc_recv.at[p, step], {'seq': partner})
 
     def finish(p):
         for step in (1, 3, 2):
             z_copies[p, step].wait_recv()
-        value = own[unit(False, True, p), :, 0:narrow] + z_in[p, 0] + z_in[p, 1] + z_in[p, 2]
-        y[:, pl.ds(column(core, side, head, p), narrow)] = value.astype(BF16)
+        value = own[unit(True, p), :, strip(head)] + z_in[p, 0] + z_in[p, 1] + z_in[p, 2]
+        y[:, pl.ds(column(core, side, p, head), narrow)] = value.astype(BF16)
         for step in (2, 1, 3):
-            gz[p, step] = spread(core, side, head, p, gz_send.at[p, step - 1], gz_recv.at[p, step - 1], {'head': lax.rem(head + step, N_HEAD)})
-        fan(head, p, 0)
+            gz[p, step] = spread(core, side, p, head, gz_send.at[p, step - 1], gz_recv.at[p, step - 1], {'head': lax.rem(head + step, N_HEAD)})
 
     def over(p):
         for step in (1, 3, 2):
             gz[p, step].wait_recv()
-            fan(lax.rem(head + N_HEAD - step, N_HEAD), p, step)
+        gy[p] = spread(core, side, p, None, gy_send.at[p], gy_recv.at[p], {'seq': across})
+        gc[p, 0] = spread(core, side, p, None, gc_send.at[p, 0], gc_recv.at[p, 0], {'seq': partner})
 
     def to_partner(p):
-        for step in (0, 1, 3, 2):
-            gy[p, step].wait_recv()
-            z = lax.rem(head + N_HEAD - step, N_HEAD)
-            gc[p, 4 + step] = spread(core, 1 - side, z, p, gc_send.at[p, 4 + step], gc_recv.at[p, 4 + step], {'seq': partner})
+        gy[p].wait_recv()
+        gc[p, 1] = spread(core, 1 - side, p, None, gc_send.at[p, 1], gc_recv.at[p, 1], {'seq': partner})
 
     stages = [(3 * p + at, n, p) for n, at in enumerate((0, 4.6, 9.3, 11.4)) for p in range(n_pass)]
     for _, n, p in sorted(stages):
@@ -404,7 +399,7 @@
         in_specs=[VMEM, VMEM, HBM],
         out_specs=VMEM,
         scratch_shapes=[
-            pltpu.VMEM((4 * n_pass, rows, N_HEAD * narrow), BF16),
+            pltpu.VMEM((rows, d_out), BF16),
             pltpu.VMEM((2, n_q, batch, LANES), F32),
             block,
             pltpu.VMEM((2, 8, LANES), F32),
@@ -417,10 +412,10 @@
             pltpu.VMEM((2 * n_pass, batch, width), F32),
             pltpu.VMEM((n_pass, batch, width), F32),
             pltpu.VMEM((n_pass, 3, batch, narrow), F32),
-            dma((4 * n_pass, N_HEAD)),
+            dma((8,)),
             dma((2, 2)), dma((2, 2)), dma((2,)), dma((2,)),
             dma((2 * n_pass,)), dma((2 * n_pass,)), dma((n_pass,)), dma((n_pass,)), dma((n_pass, 3)), dma((n_pass, 3)),
-            dma((n_pass, 3)), dma((n_pass, 3)), dma((n_pass, 4)), dma((n_pass, 4)), dma((n_pass, 8)), dma((n_pass, 8)),
+            dma((n_pass, 3)), dma((n_pass, 3)), dma((n_pass,)), dma((n_pass,)), dma((n_pass, 2)), dma((n_pass, 2)),
         ],
         compiler_params=pltpu.CompilerParams(collective_id=1, has_side_effects=True, vmem_limit_bytes=24 * 2**20),
         name='output',

time: 65.1 us -> 65.2 us (level)
  no operation moved by 1% of the time
where the time goes in v5:
time: 65.2 us; the launch traced here: 65 us
  Pallas kernels  63.4 us (97%)
  local copies, waits for them, and re-layouts  0.98 us (2%)
  between operations  0.67 us (1%)
    pallas_call x1, Pallas kernels, output(): pl.pallas_call(functools.partial(output_kernel, n_pass), out_shape=pltpu....  44.9 us
    pallas_call x1, Pallas kernels, project(): pl.pallas_call(functools.partial(project_kernel, n_chunk, 8), out_shape=[...  11 us
    pallas_call x1, Pallas kernels, attend(): pl.pallas_call(functools.partial(attend_kernel, n_chunk, shard_len), out_...  7.47 us

profile of v5, /device:TPU:0, one launch (start us, length us, event | category | flops | bytes accessed | tf_op | source)
XLA Modules:
  0.0 65.0 jit_solution(10388547564322485064)
XLA Ops:
  0.6 0.0 copy-start
  0.6 11.0 %project.1 = (bf16[4,5,64,128]{3,2,1,0:T(8,128)(2,1)S(1)}, bf16[64,512,128]{2,1,0:T(8,128)(2,1)S(1)}, bf16[64,512,128]{2,1,0:T(8,128)(2,1)S(1)}) custom-call(bf16[64,8192]{1,0:T(8,128)(2,1)} %tok_hbm.1, bf16[8192,8192]{1,0:T(8,128)(2,1)} %wq_hbm.1, bf16[8192,1024]{1,0:T(8,128)(2,1)} %wk_hbm.1, bf16[8192,1024]{1,0:T(8,128)(2,1)} %wv_hbm.1, ...), custom_call_target="tpu_custom_call" | custom-call | tf_op jit(solution)/shard_map/project/pallas_call | solution.py:132
  11.6 0.0 copy-done
  11.6 7.5 %attend.1 = (bf16[64,512,128]{2,1,0:T(8,128)(2,1)}, bf16[64,512,128]{2,1,0:T(8,128)(2,1)}, f32[1024,128]{1,0:T(8,128)S(1)}, f32[4,8,128]{2,1,0:T(8,128)S(1)}, bf...) custom-call(s32[64]{0:T(128)S(1)} %copy-done, ...), custom_call_target="tpu_custom_call", output_to_operand_aliasing={{4}: (2, {}), {5}: (3, {})} | custom-call | tf_op jit(solution)/shard_map/attend/pallas_call | solution.py:225
  19.1 44.9 %output.1 = bf16[64,8192]{1,0:T(8,128)(2,1)S(1)} custom-call(f32[16,64,128]{2,1,0:T(8,128)S(1)} %bitcast.5, f32[4,8,128]{2,1,0:T(8,128)S(1)} %get-tuple-element.14.ml, bf16[512,8192]{1,0:T(8,128)(2,1)} %wo_hbm.1), custom_call_target="tpu_custom_call" | custom-call | tf_op jit(solution)/shard_map/output/pallas_call | solution.py:396
  64.1 1.0 %copy.16 = bf16[64,8192]{1,0:T(8,128)(2,1)} copy(bf16[64,8192]{1,0:T(8,128)(2,1)S(1)} %output.1) | data formatting | bytes 2097152
Async XLA Ops:
  0.6 11.0 %copy-start = (s32[64]{0:T(128)S(1)}, s32[64]{0:T(128)}, u32[]{:S(2)}) copy-start(s32[64]{0:T(128)} %pos_ref.1) | copy-start | bytes 772

commit v6 on v5

--- a/solution.py
+++ b/solution.py
@@ -251,7 +251,7 @@
     return top, total, factors
 
 
-def output_kernel(n_pass, mix, ml, wo_hbm, y, wo, pair_in, far_in, pair_ml, far_ml, far_give, far_give_ml, attn, give, own, core_in, y_in, z_in,
+def output_kernel(n_pass, mix, ml, wo_hbm, y, wo, pair_in, far_in, pair_ml, far_ml, far_give, far_give_ml, attn, give, own, core_in, y_in, z_in, whole,
                   wo_sem, p_send, p_recv, f_send, f_recv, c_send, c_recv, y_send, y_recv, z_send, z_recv,
                   gz_send, gz_recv, gy_send, gy_recv, gc_send, gc_recv):
     head, seq = lax.axis_index('head'), lax.axis_index('seq')
@@ -263,12 +263,8 @@
     narrow = z_in.shape[3]
     wait_peers = entry_barrier((('seq', N_SEQ), ('head', N_HEAD)))
 
-    def column(half, quarter, p, z=None):
-        at = ((half * 2 + quarter) * n_pass + p) * N_HEAD * narrow
-        return pl.multiple_of(at if z is None else at + z * narrow, narrow)
-
-    def strip(z):
-        return pl.ds(pl.multiple_of(z * narrow, narrow), narrow)
+    def place(half, quarter, p):
+        return (half * 2 + quarter) * n_pass + p
 
     def unit(near, p):
         return (1 if near else 0) * n_pass + p
@@ -316,19 +312,22 @@
         copy.wait()
 
     def partial(half, near, p):
-        at = column(half, side if near else 1 - side, p)
-        return jnp.dot(attn[...], wo[:, pl.ds(at, N_HEAD * narrow)], preferred_element_type=F32)
+        at = pl.multiple_of(place(half, side if near else 1 - side, p) * N_HEAD * narrow, narrow)
+        value = jnp.dot(attn[...], wo[:, pl.ds(at, N_HEAD * narrow)], preferred_element_type=F32)
+        return [value[:, z * narrow:(z + 1) * narrow] for z in range(N_HEAD)]
 
     def hand(near, p):
         u = unit(near, p)
-        give[u] = partial(1 - core, near, p)
+        for z, value in enumerate(partial(1 - core, near, p)):
+            give[u, z] = value
         c_copies[u] = remote(give.at[u], core_in.at[u], c_send.at[u], c_recv.at[u], {'seq': partner})
 
     def keep(near, p):
         u = unit(near, p)
-        value = partial(core, near, p)
+        values = partial(core, near, p)
         c_copies[u].wait_recv()
-        own[u] = value + core_in[u]
+        for z, value in enumerate(values):
+            own[u, z] = value + core_in[u, z]
 
     c_copies, y_copies, z_copies = {}, {}, {}
     for p in range(n_pass):
@@ -347,11 +346,10 @@
         own[u] = own[u] + y_in[p]
         for step in (2, 1, 3):
             to = lax.rem(head + step, N_HEAD)
-            z_copies[p, step] = remote(own.at[u, :, strip(to)], z_in.at[p, step - 1], z_send.at[p, step - 1], z_recv.at[p, step - 1],
+            z_copies[p, step] = remote(own.at[u, to], z_in.at[p, step - 1], z_send.at[p, step - 1], z_recv.at[p, step - 1],
                                        {'head': to})
 
-    def spread(half, quarter, p, z, send, recv, device):
-        at = y.at[:, pl.ds(column(half, quarter, p, z), narrow if z is not None else N_HEAD * narrow)]
+    def spread(at, send, recv, device):
         return remote(at, at, send, recv, device)
 
     gz, gy, gc = {}, {}, {}
@@ -359,26 +357,30 @@
     def finish(p):
         for step in (1, 3, 2):
             z_copies[p, step].wait_recv()
-        value = own[unit(True, p), :, strip(head)] + z_in[p, 0] + z_in[p, 1] + z_in[p, 2]
-        y[:, pl.ds(column(core, side, p, head), narrow)] = value.astype(BF16)
+        at = place(core, side, p)
+        whole[at, head] = (own[unit(True, p), head] + z_in[p, 0] + z_in[p, 1] + z_in[p, 2]).astype(BF16)
         for step in (2, 1, 3):
-            gz[p, step] = spread(core, side, p, head, gz_send.at[p, step - 1], gz_recv.at[p, step - 1], {'head': lax.rem(head + step, N_HEAD)})
+            gz[p, step] = spread(whole.at[at, head], gz_send.at[p, step - 1], gz_recv.at[p, step - 1], {'head': lax.rem(head + step, N_HEAD)})
 
     def over(p):
         for step in (1, 3, 2):
             gz[p, step].wait_recv()
-        gy[p] = spread(core, side, p, None, gy_send.at[p], gy_recv.at[p], {'seq': across})
-        gc[p, 0] = spread(core, side, p, None, gc_send.at[p, 0], gc_recv.at[p, 0], {'seq': partner})
+        at = whole.at[place(core, side, p)]
+        gy[p] = spread(at, gy_send.at[p], gy_recv.at[p], {'seq': across})
+        gc[p, 0] = spread(at, gc_send.at[p, 0], gc_recv.at[p, 0], {'seq': partner})
 
     def to_partner(p):
         gy[p].wait_recv()
-        gc[p, 1] = spread(core, 1 - side, p, None, gc_send.at[p, 1], gc_recv.at[p, 1], {'seq': partner})
+        gc[p, 1] = spread(whole.at[place(core, 1 - side, p)], gc_send.at[p, 1], gc_recv.at[p, 1], {'seq': partner})
 
     stages = [(3 * p + at, n, p) for n, at in enumerate((0, 4.6, 9.3, 11.4)) for p in range(n_pass)]
     for _, n, p in sorted(stages):
         (along, finish, over, to_partner)[n](p)
     for copy in gc.values():
         copy.wait_recv()
+    for u in range(whole.shape[0]):
+        for z in range(N_HEAD):
+            y[:, (u * N_HEAD + z) * narrow:(u * N_HEAD + z + 1) * narrow] = whole[u, z]
     for group in (sends, *(g.values() for g in (c_copies, y_copies, z_copies, gz, gy, gc))):
         for copy in group:
             copy.wait_send()
@@ -407,11 +409,12 @@
             block,
             pltpu.VMEM((8, LANES), F32),
             pltpu.VMEM((batch, rows), BF16),
-            pltpu.VMEM((2 * n_pass, batch, width), F32),
-            pltpu.VMEM((2 * n_pass, batch, width), F32),
-            pltpu.VMEM((2 * n_pass, batch, width), F32),
-            pltpu.VMEM((n_pass, batch, width), F32),
+            pltpu.VMEM((2 * n_pass, N_HEAD, batch, narrow), F32),
+            pltpu.VMEM((2 * n_pass, N_HEAD, batch, narrow), F32),
+            pltpu.VMEM((2 * n_pass, N_HEAD, batch, narrow), F32),
+            pltpu.VMEM((n_pass, N_HEAD, batch, narrow), F32),
             pltpu.VMEM((n_pass, 3, batch, narrow), F32),
+            pltpu.VMEM((4 * n_pass, N_HEAD, batch, narrow), BF16),
             dma((8,)),
             dma((2, 2)), dma((2, 2)), dma((2,)), dma((2,)),
             dma((2 * n_pass,)), dma((2 * n_pass,)), dma((n_pass,)), dma((n_pass,)), dma((n_pass, 3)), dma((n_pass, 3)),

time: 65.2 us -> 65.5 us (level)
  no operation moved by 1% of the time
where the time goes in v6:
time: 65.5 us; the launch traced here: 65.2 us
  Pallas kernels  63.6 us (97%)
  local copies, waits for them, and re-layouts  0.98 us (1%)
  between operations  0.67 us (1%)
    pallas_call x1, Pallas kernels, output(): pl.pallas_call(functools.partial(output_kernel, n_pass), out_shape=pltpu....  45.1 us
    pallas_call x1, Pallas kernels, project(): pl.pallas_call(functools.partial(project_kernel, n_chunk, 8), out_shape=[...  11 us
    pallas_call x1, Pallas kernels, attend(): pl.pallas_call(functools.partial(attend_kernel, n_chunk, shard_len), out_...  7.47 us

profile of v6, /device:TPU:0, one launch (start us, length us, event | category | flops | bytes accessed | tf_op | source)
XLA Modules:
  0.0 65.2 jit_solution(1209747658007086775)
XLA Ops:
  0.6 0.0 copy-start
  0.6 11.0 %project.1 = (bf16[4,5,64,128]{3,2,1,0:T(8,128)(2,1)S(1)}, bf16[64,512,128]{2,1,0:T(8,128)(2,1)S(1)}, bf16[64,512,128]{2,1,0:T(8,128)(2,1)S(1)}) custom-call(bf16[64,8192]{1,0:T(8,128)(2,1)} %tok_hbm.1, bf16[8192,8192]{1,0:T(8,128)(2,1)} %wq_hbm.1, bf16[8192,1024]{1,0:T(8,128)(2,1)} %wk_hbm.1, bf16[8192,1024]{1,0:T(8,128)(2,1)} %wv_hbm.1, ...), custom_call_target="tpu_custom_call" | custom-call | tf_op jit(solution)/shard_map/project/pallas_call | solution.py:132
  11.6 0.0 copy-done
  11.6 7.5 %attend.1 = (bf16[64,512,128]{2,1,0:T(8,128)(2,1)}, bf16[64,512,128]{2,1,0:T(8,128)(2,1)}, f32[1024,128]{1,0:T(8,128)S(1)}, f32[4,8,128]{2,1,0:T(8,128)S(1)}, bf...) custom-call(s32[64]{0:T(128)S(1)} %copy-done, ...), custom_call_target="tpu_custom_call", output_to_operand_aliasing={{4}: (2, {}), {5}: (3, {})} | custom-call | tf_op jit(solution)/shard_map/attend/pallas_call | solution.py:225
  19.1 45.1 %output.1 = bf16[64,8192]{1,0:T(8,128)(2,1)S(1)} custom-call(f32[16,64,128]{2,1,0:T(8,128)S(1)} %bitcast.5, f32[4,8,128]{2,1,0:T(8,128)S(1)} %get-tuple-element.14.ml, bf16[512,8192]{1,0:T(8,128)(2,1)} %wo_hbm.1), custom_call_target="tpu_custom_call" | custom-call | tf_op jit(solution)/shard_map/output/pallas_call | solution.py:398
  64.3 1.0 %copy.16 = bf16[64,8192]{1,0:T(8,128)(2,1)} copy(bf16[64,8192]{1,0:T(8,128)(2,1)S(1)} %output.1) | data formatting | bytes 2097152
Async XLA Ops:
  0.6 11.0 %copy-start = (s32[64]{0:T(128)S(1)}, s32[64]{0:T(128)}, u32[]{:S(2)}) copy-start(s32[64]{0:T(128)} %pos_ref.1) | copy-start | bytes 772
